TPU v7x, 128 devices: a whole 4x4x4 slice. The times are simulated.
128 devices in a mesh: dp: 1, ep: 128 (over z, y, x, core).
Axes of the slice: x: 4, y: 4, z: 4, core: 2. Of those that a mesh axis runs over, the one named last changes fastest.
Arguments:
- x_in: bfloat16 [32768, 2048], P(('dp', 'ep'))
- norm_gain: bfloat16 [2048], replicated
- w_router: bfloat16 [2048, 128], replicated
- expert_ids: int32 [32768, 8], P(('dp', 'ep'))
- w_gate: bfloat16 [128, 2048, 768], P('ep')
- w_up: bfloat16 [128, 2048, 768], P('ep')
- w_down: bfloat16 [128, 768, 2048], P('ep')
Outputs:
- output: bfloat16 [32768, 2048], P(('dp', 'ep'))
All inputs are finite; a program needn't handle non-finite values.
Results may differ from a plain program's by a relative error of at most 0.00693909.
Values are sent between devices in bfloat16 or wider.
A program may use at most 1 GiB of HBM per device.

v0:
```python
import jax
import jax.numpy as jnp
from jax import lax
from jax.sharding import PartitionSpec as P

EPS = 1e-6


def norm_and_gates(x_in, norm_gain, w_router, expert_ids):
    resid = x_in.astype(jnp.float32)
    mean_sq = jnp.mean(resid * resid, axis=-1, keepdims=True)
    normed = (resid * lax.rsqrt(mean_sq + EPS) * norm_gain.astype(jnp.float32)).astype(jnp.bfloat16)
    logits = jnp.dot(normed, w_router, preferred_element_type=jnp.float32)
    router_p = jax.nn.softmax(logits, axis=-1)
    picked = jnp.take_along_axis(router_p, expert_ids, axis=1)
    gates = picked / jnp.sum(picked, axis=1, keepdims=True)
    return resid, normed, gates


def route_slots(expert_ids, experts, capacity):
    flat_ids = expert_ids.reshape(-1)
    onehot = (flat_ids[:, None] == jnp.arange(experts, dtype=jnp.int32)[None, :]).astype(jnp.int32)
    before = jnp.cumsum(onehot, axis=0) - onehot
    position = jnp.sum(before * onehot, axis=1)
    return flat_ids * capacity + position


def expert_mlp(rows, w_gate, w_up, w_down):
    gate_val = jnp.einsum("erd,edf->erf", rows, w_gate, preferred_element_type=jnp.float32)
    up_val = jnp.einsum("erd,edf->erf", rows, w_up, preferred_element_type=jnp.float32)
    hidden_act = (jax.nn.silu(gate_val) * up_val).astype(jnp.bfloat16)
    return jnp.einsum("erf,efd->erd", hidden_act, w_down, preferred_element_type=jnp.float32).astype(jnp.bfloat16)


def solution(mesh):
    def local_block(x_in, norm_gain, w_router, expert_ids, w_gate, w_up, w_down):
        tokens, hidden = x_in.shape
        experts = w_router.shape[1]
        top_k = expert_ids.shape[1]
        capacity = 2 * tokens * top_k // experts
        resid, normed, gates = norm_and_gates(x_in, norm_gain, w_router, expert_ids)
        slots = route_slots(expert_ids, experts, capacity)
        choice_tok = jnp.arange(tokens * top_k, dtype=jnp.int32) // top_k
        slot_tok = jnp.full((experts * capacity,), tokens, jnp.int32).at[slots].set(choice_tok)
        outgoing = jnp.take(normed, slot_tok, axis=0, mode="fill", fill_value=0).reshape(experts, capacity, hidden)
        received = lax.all_to_all(outgoing, "ep", 0, 1, tiled=True)
        outputs = expert_mlp(received, w_gate, w_up, w_down)
        returned = lax.all_to_all(outputs, "ep", 1, 0, tiled=True).reshape(experts * capacity, hidden)
        y_sel = jnp.take(returned, slots, axis=0).reshape(tokens, top_k, hidden)
        mixed = jnp.sum(y_sel.astype(jnp.float32) * gates[:, :, None], axis=1)
        return (resid + mixed).astype(jnp.bfloat16)

    tok_spec = P(("dp", "ep"), None)
    expert_spec = P("ep", None, None)
    return jax.shard_map(local_block, mesh=mesh, in_specs=(tok_spec, P(None), P(None, None), tok_spec, expert_spec, expert_spec, expert_spec), out_specs=tok_spec, check_vma=False)
```

profile of v0, /device:TPU:2, one launch (start us, length us, event | category | flops | bytes accessed | tf_op | source)
XLA Modules:
  0.0 900.5 jit_solution(4947991075179443954)
XLA Ops:
  0.0 0.0 copy-start
  0.0 0.9 broadcast_multiply_fusion
  0.9 0.9 copy.42
  1.8 0.1 eq.26
  1.9 0.1 reshape.143
  2.0 0.1 copy.48
  2.1 0.1 mul.61
  2.3 0.1 copy.44
  2.4 0.3 fusion.11
  2.7 0.0 copy-start.4
  2.7 1.0 copy-done.4
  3.7 1.3 broadcast_add_fusion
  5.0 0.3 copy.45
  5.4 0.6 fusion.10
  6.0 0.0 copy-start.7
  6.0 0.6 copy-done.7
  6.6 0.0 copy-start.9
  6.6 8.1 scatter_custom_fusion
  14.7 0.0 copy-done.9
  14.7 1.5 fusion.5
  16.2 0.7 convert_element_type.35
  16.9 0.1 broadcast_in_dim.41
  17.0 2.5 fusion.7
  19.5 32.7 %gather_fusion = bf16[4096,2048]{1,0:T(8,128)(2,1)} fusion(bf16[256,2048]{1,0:T(8,128)(2,1)} %fusion.7, s32[4096]{0:T(1024)S(1)} %fusion.16), kind=kCustom, calls=%fused_computation | custom fusion | bytes 33570816 | tf_op jit(solution)/shard_map/jit(_take)/gather | solution.py:45
  52.2 8.3 broadcast_select_fusion
  60.5 0.0 copy-start.11
  60.5 224.0 %all_to_all.8 = bf16[128,32,2048]{2,1,0:T(8,128)(2,1)S(1)} all-to-all(bf16[128,32,2048]{2,1,0:T(8,128)(2,1)S(1)} %broadcast_select_fusion), channel_id=1, replica_groups=mesh['dp'=1,'ep'=128] {'ep'}, dimensions={0} | all-to-all | bytes 33554432 | tf_op jit(solution)/shard_map/all_to_all | solution.py:46
  284.5 5.7 copy-done.3
  290.2 0.0 copy-done.11
  290.2 16.3 %fusion.3 = f32[4096,768]{1,0:T(8,128)} fusion(bf16[4096,2048]{1,0:T(8,128)(2,1)S(1)} %bitcast.50, bf16[1,2048,768]{2,1,0:T(8,128)(2,1)S(1)} %copy-done.11), kind=kOutput, calls=%fused_computation.12 | convolution fusion | flops 12884901888 | bytes 32505856 | tf_op jit(solution)/shard_map/erd,edf->erf/dot_general | solution.py:29
  306.5 0.0 copy-done
  306.5 36.5 %convert_bitcast_fusion = bf16[1,4096,2048]{2,1,0:T(8,128)(2,1)} fusion(f32[4096,768]{1,0:T(8,128)} %fusion.3, bf16[4096,2048]{1,0:T(8,128)(2,1)} %bitcast.51, bf16[1,768,2048]{2,1,0:T(8,128)(2,1)S(1)} %copy-done, bf16[1,2048,768]{2,1,0:T(8,128)(2,1)} %param.12), kind=kOutput, calls=%fused_computation.6 | convolution fusion | flops 25797066752 | bytes 52428800 | tf_op jit(solution)/shard_map/erf,efd->erd/dot_general | solution.py:32
  343.0 29.2 %copy.57 = bf16[1,4096,2048]{2,0,1:T(2,128)(2,1)} copy(bf16[1,4096,2048]{2,1,0:T(8,128)(2,1)} %convert_bitcast_fusion) | data formatting | bytes 33554432 | tf_op jit(solution)/shard_map/convert_element_type | solution.py:32
  372.2 0.6 broadcast.132
  372.8 99.6 %reduce = bf16[4096,2048]{1,0:T(8,128)(2,1)} reduce(bf16[4096,1,2048]{2,1,0:T(2,128)(2,1)} %bitcast.47, bf16[]{:T(256)} %broadcast.132), dimensions={1}, to_apply=%bitcast.44.reduce_sub_computation | reduce | bytes 33554432
  472.3 27.7 %reshape.189 = bf16[128,2,32768]{2,1,0:T(2,128)(2,1)} reshape(bf16[4096,2048]{1,0:T(8,128)(2,1)} %reduce) | data formatting | bytes 33554432
  500.1 0.0 copy-start.8
  500.1 0.0 copy-start.6
  500.1 0.0 copy-start.2
  500.1 0.0 copy-start.5
  500.1 14.8 %all-to-all-start.1 = ((bf16[128,2,32768]{2,1,0:T(2,128)(2,1)}), bf16[128,2,32768]{2,1,0:T(2,128)(2,1)}, u32[]{:S(2)}, u32[]{:S(2)}) async-start(bf16[128,2,32768]{2,1,0:T(2,128)(2,1)} %reshape.189), calls=%async_computation.1 | async-start | bytes 33554432 | tf_op jit(solution)/shard_map/all_to_all | solution.py:48
  514.9 0.0 copy-done.8
  514.9 0.1 reduce_sum.50
  515.0 0.0 copy-done.6
  515.0 0.1 copy.50
  515.1 0.1 reshape.167
  515.2 0.1 copy.46
  515.3 0.2 copy.47
  515.5 0.0 copy-done.2
  515.5 0.0 copy-done.5
  515.5 0.5 fusion.24
  516.1 0.0 copy-start.10
  516.1 16.8 %gather_fusion.2 = f32[2048]{0:T(1024)S(1)} fusion(f32[256,128]{0,1:T(8,128)S(1)} %fusion.14, s32[2048]{0:T(1024)S(1)} %reshape.167), kind=kCustom, calls=%fused_computation.2 | custom fusion | bytes 32768 | tf_op jit(solution)/shard_map/jit(take_along_axis)/gather | solution.py:15
  532.9 0.1 reshape.170
  533.0 0.1 copy.51
  533.1 0.1 copy.52
  533.3 0.0 copy-done.10
  533.3 230.9 %all-to-all-done.1 = bf16[128,2,32768]{2,1,0:T(2,128)(2,1)} async-done(((bf16[128,2,32768]{2,1,0:T(2,128)(2,1)}), bf16[128,2,32768]{2,1,0:T(2,128)(2,1)}, u32[]{:S(2)}, u32[]{:S(2)}) %all-to-all-start.1) | async-done | bytes 16777248 | tf_op jit(solution)/shard_map/all_to_all | solution.py:48
  764.2 75.6 %reshape.190 = bf16[4096,1,2048]{2,1,0:T(2,128)(2,1)} reshape(bf16[128,2,32768]{2,1,0:T(2,128)(2,1)} %all-to-all-done.1) | data formatting | bytes 33554432
  839.8 24.1 %copy.56 = bf16[1,4096,2048]{2,1,0:T(8,128)(2,1)} copy(bf16[1,4096,2048]{2,0,1:T(2,128)(2,1)} %bitcast.48) | data formatting | bytes 33554432
  863.9 24.4 %gather_fusion.1 = bf16[2048,2048]{1,0:T(8,128)(2,1)} fusion(bf16[4096,2048]{1,0:T(8,128)(2,1)} %bitcast.46, s32[2048]{0:T(1024)S(1)} %broadcast_clamp_fusion), kind=kCustom, calls=%fused_computation.1 | custom fusion | bytes 16785408 | tf_op jit(solution)/shard_map/jit(_take)/gather | solution.py:49
  888.3 9.6 %multiply_reduce_fusion = f32[256,2048]{1,0:T(8,128)S(1)} fusion(bf16[2048,2048]{1,0:T(8,128)(2,1)} %gather_fusion.1, f32[256,8]{1,0:T(8,128)S(1)} %copy.52, pred[256,8]{1,0:T(8,128)(4,1)S(1)} %copy.47), kind=kLoop, calls=%fused_computation.5 | loop fusion | flops 16252928 | bytes 10496000 | tf_op jit(solution)/shard_map/reduce_sum | solution.py:50
  897.9 2.5 fusion.8
  900.5 0.0 copy-done.1
  (17 shorter events, 0.2 us)
Async XLA Ops:
  0.0 306.5 %copy-start = (bf16[1,768,2048]{2,1,0:T(8,128)(2,1)S(1)}, bf16[1,768,2048]{2,1,0:T(8,128)(2,1)}, u32[]{:S(2)}) copy-start(bf16[1,768,2048]{2,1,0:T(8,128)(2,1)} %param.13) | copy-start | bytes 9437188
  2.7 1.0 copy-start.4
  6.0 0.6 copy-start.7
  6.6 8.1 copy-start.9
  60.5 229.8 %copy-start.11 = (bf16[1,2048,768]{2,1,0:T(8,128)(2,1)S(1)}, bf16[1,2048,768]{2,1,0:T(8,128)(2,1)}, u32[]{:S(2)}) copy-start(bf16[1,2048,768]{2,1,0:T(8,128)(2,1)} %param.11) | copy-start | bytes 9437188
  284.5 5.7 copy-start.3
  500.1 14.8 %copy-start.8 = (s32[2048]{0:T(1024)S(1)}, s32[2048]{0:T(1024)}, u32[]{:S(2)}) copy-start(s32[2048]{0:T(1024)} %copy-done.7) | copy-start | bytes 24580
  500.1 14.9 %copy-start.6 = (s32[256,8]{0,1:T(8,128)S(1)}, s32[256,8]{0,1:T(8,128)}, u32[]{:S(2)}) copy-start(s32[256,8]{0,1:T(8,128)} %param.10) | copy-start | bytes 24580
  500.1 15.4 %copy-start.2 = (bf16[256,2048]{1,0:T(8,128)(2,1)S(1)}, bf16[256,2048]{1,0:T(8,128)(2,1)}, u32[]{:S(2)}) copy-start(bf16[256,2048]{1,0:T(8,128)(2,1)} %fusion.7) | copy-start | bytes 3145732
  500.1 15.4 %copy-start.5 = (bf16[2048,128]{1,0:T(8,128)(2,1)S(1)}, bf16[2048,128]{1,0:T(8,128)(2,1)}, u32[]{:S(2)}) copy-start(bf16[2048,128]{1,0:T(8,128)(2,1)} %param.9) | copy-start | bytes 1572868
  500.1 264.1 %all-to-all-start.1 = ((bf16[128,2,32768]{2,1,0:T(2,128)(2,1)}), bf16[128,2,32768]{2,1,0:T(2,128)(2,1)}, u32[]{:S(2)}, u32[]{:S(2)}) async-start(bf16[128,2,32768]{2,1,0:T(2,128)(2,1)} %reshape.189), calls=%async_computation.1 | async-start | bytes 33554432 | tf_op jit(solution)/shard_map/all_to_all | solution.py:48
  516.1 17.1 %copy-start.10 = (s32[2048,1]{0,1:T(1,128)S(1)}, s32[2048,1]{0,1:T(1,128)}, u32[]{:S(2)}) copy-start(s32[2048,1]{0,1:T(1,128)} %copy-done.9) | copy-start | bytes 24580
  863.9 36.6 %copy-start.1 = (bf16[1,768,2048]{2,1,0:T(8,128)(2,1)S(1)}, bf16[1,768,2048]{2,1,0:T(8,128)(2,1)}, u32[]{:S(2)}) copy-start(bf16[1,768,2048]{2,1,0:T(8,128)(2,1)} %param.13) | copy-start | bytes 9437188
where the time goes:
time: 904 us; the launch traced here: 900 us
  local copies, waits for them, and re-layouts  249 us (28%)
  waiting for transfers between devices  231 us (26%)
  blocking collectives  224 us (25%)
  other arithmetic  128 us (14%)
  matrix products  53.3 us (6%)
  starting transfers between devices  14.8 us (2%)
    all_to_all x1, waiting for transfers between devices, local_block(): lax.all_to_all(outputs, 'ep', 1, 0, tiled=True)  231 us
    all_to_all x1, blocking collectives, local_block(): received = lax.all_to_all(outgoing, 'ep', 0, 1, tiled=True)  224 us
    unnamed x29, local copies, waits for them, and re-layouts  136 us
    unnamed x1, other arithmetic  99.6 us
    dot_general x1, matrix products, expert_mlp(): jnp.einsum('erf,efd->erd', hidden_act, w_down, preferred_element_type=jnp...  36.5 us
    gather x1, local copies, waits for them, and re-layouts, local_block(): jnp.take(normed, slot_tok, axis=0, mode='fill', fill_value=0)  32.7 us
    convert_element_type x1, local copies, waits for them, and re-layouts, expert_mlp(): jnp.einsum('erf,efd->erd', hidden_act, w_down, preferred_element_type=jnp...  29.2 us
    gather x1, local copies, waits for them, and re-layouts, local_block(): y_sel = jnp.take(returned, slots, axis=0).reshape(tokens, top_k, hidden)  24.4 us
  transfers between devices with their start and end apart: 1, of which 1 were waited for; matrix products, arithmetic and copies ran while one was open for 2% of the time, Pallas kernels for 0%

commit v1 on v0

v1 whole, which is shorter than its diff:
```python
import functools

import jax
import jax.numpy as jnp
from jax import lax
from jax.experimental import pallas as pl
from jax.experimental.pallas import tpu as pltpu
from jax.sharding import PartitionSpec as P

EPS = 1e-6
SLOTS = 32
F32, BF16 = jnp.float32, jnp.bfloat16


def route_kernel(x_ref, gain_ref, wr_ref, ids_ref, idst_ref, h_ref, gate_ref, pos_ref, post_ref):
    tokens, experts = gate_ref.shape[1], gate_ref.shape[2]
    top_k = ids_ref.shape[1]
    resid = x_ref[...].astype(F32)
    mean_sq = jnp.mean(resid * resid, axis=-1, keepdims=True)
    normed = (resid * lax.rsqrt(mean_sq + EPS) * gain_ref[...].astype(F32)).astype(BF16)
    h_ref[...] = normed
    logits = jnp.dot(normed, wr_ref[...], preferred_element_type=F32)
    exps = jnp.exp(logits - jnp.max(logits, axis=-1, keepdims=True))
    router_p = exps / jnp.sum(exps, axis=-1, keepdims=True)

    lane_expert = lax.broadcasted_iota(jnp.int32, (tokens, experts), 1)
    chosen = jnp.zeros((tokens, experts), F32)
    row_expert = lax.broadcasted_iota(jnp.int32, (experts, tokens), 0)
    chosen_t = jnp.zeros((experts, tokens), F32)
    for j in range(top_k):
        chosen += jnp.where(ids_ref[:, j:j + 1] == lane_expert, 1.0, 0.0)
        chosen_t += jnp.where(idst_ref[j:j + 1, :] == row_expert, 1.0, 0.0)

    picked = router_p * chosen
    gates = picked / jnp.sum(picked, axis=-1, keepdims=True)
    part0 = gates.astype(BF16)
    rest = gates - part0.astype(F32)
    part1 = rest.astype(BF16)
    part2 = (rest - part1.astype(F32)).astype(BF16)
    gate_ref[0] = part0
    gate_ref[1] = part1
    gate_ref[2] = part2

    rows = lax.broadcasted_iota(jnp.int32, (tokens, tokens), 0)
    cols = lax.broadcasted_iota(jnp.int32, (tokens, tokens), 1)
    lower = jnp.where(cols < rows, 1.0, 0.0).astype(BF16)
    upper = jnp.where(rows < cols, 1.0, 0.0).astype(BF16)
    pos = jnp.dot(lower, chosen.astype(BF16), preferred_element_type=F32)
    pos_t = jnp.dot(chosen_t.astype(BF16), upper, preferred_element_type=F32)
    pos_ref[...] = jnp.where(chosen > 0.0, pos, 255.0).astype(BF16)
    post_ref[...] = jnp.where(chosen_t > 0.0, pos_t, 255.0)


def pack_kernel(slots, h_ref, post_ref, out_ref):
    group, tokens = post_ref.shape
    slot = lax.broadcasted_iota(jnp.int32, (group, slots, tokens), 1).astype(F32)
    pick = jnp.where(post_ref[...][:, None, :] == slot, 1.0, 0.0).astype(BF16)
    rows = jnp.dot(pick.reshape(group * slots, tokens), h_ref[...], preferred_element_type=F32).astype(BF16)
    out_ref[...] = rows


def mlp_kernel(x_ref, wg_ref, wu_ref, wd_ref, y_ref):
    rows = x_ref[...]
    gate_val = jnp.dot(rows, wg_ref[0], preferred_element_type=F32)
    up_val = jnp.dot(rows, wu_ref[0], preferred_element_type=F32)
    act = (jax.nn.silu(gate_val) * up_val).astype(BF16)
    y_ref[...] = jnp.dot(act, wd_ref[0], preferred_element_type=F32).astype(BF16)


def combine_kernel(slots, gate_ref, pos_ref, y_ref, base_ref, out_ref, acc_ref):
    step = pl.program_id(0)
    width = y_ref.shape[0]
    tokens, experts = pos_ref.shape

    @pl.when(step == 0)
    def _():
        acc_ref[...] = base_ref[...].astype(F32)

    expert = lax.broadcasted_iota(jnp.int32, (experts, width), 0)
    column = lax.broadcasted_iota(jnp.int32, (experts, width), 1) + step * width
    spread = jnp.where(column // slots == expert, 1.0, 0.0).astype(BF16)
    gates = gate_ref[...].reshape(3 * tokens, experts)
    wide_gate = jnp.dot(gates, spread, preferred_element_type=F32).reshape(3, tokens, width)
    wide_pos = jnp.dot(pos_ref[...], spread, preferred_element_type=F32)
    slot = (lax.broadcasted_iota(jnp.int32, (tokens, width), 1) % slots).astype(F32)
    hit = (wide_pos == slot)[None]
    weight = jnp.where(hit, wide_gate, 0.0).astype(BF16).reshape(3 * tokens, width)
    sums = jnp.dot(weight, y_ref[...], preferred_element_type=F32)
    acc_ref[...] += sums[:tokens] + sums[tokens:2 * tokens] + sums[2 * tokens:]

    @pl.when(step == pl.num_programs(0) - 1)
    def _():
        out_ref[...] = acc_ref[...].astype(out_ref.dtype)


def params(**kw):
    return pltpu.CompilerParams(vmem_limit_bytes=60 * 2 ** 20, **kw)


def cost(flops, nbytes):
    return pl.CostEstimate(flops=int(flops), bytes_accessed=int(nbytes), transcendentals=0)


def route(x_in, norm_gain, w_router, expert_ids):
    tokens, hidden = x_in.shape
    experts = w_router.shape[1]
    shape = jax.ShapeDtypeStruct
    return pl.pallas_call(
        route_kernel,
        out_shape=(shape((tokens, hidden), BF16), shape((3, tokens, experts), BF16), shape((tokens, experts), BF16), shape((experts, tokens), F32)),
        compiler_params=params(),
        cost_estimate=cost(2 * tokens * hidden * experts, 4 * tokens * hidden),
        name="route",
    )(x_in, norm_gain.reshape(1, hidden), w_router, expert_ids, expert_ids.T)


def pack(h, pos_t, slots, group):
    tokens, hidden = h.shape
    experts = pos_t.shape[0]
    return pl.pallas_call(
        functools.partial(pack_kernel, slots),
        grid=(experts // group,),
        out_shape=jax.ShapeDtypeStruct((experts * slots, hidden), BF16),
        in_specs=[pl.BlockSpec((tokens, hidden), lambda i: (0, 0)), pl.BlockSpec((group, tokens), lambda i: (i, 0))],
        out_specs=pl.BlockSpec((group * slots, hidden), lambda i: (i, 0)),
        compiler_params=params(),
        cost_estimate=cost(2 * experts * slots * tokens * hidden, 2 * experts * slots * hidden),
        name="pack",
    )(h, pos_t)


def exchange(rows, devices):
    blocks = rows.reshape(devices, rows.shape[0] // devices, rows.shape[1])
    return lax.all_to_all(blocks, "ep", 0, 0, tiled=True).reshape(rows.shape)


def mlp(rows, w_gate, w_up, w_down, block):
    total, hidden = rows.shape
    ff = w_gate.shape[2]
    whole = lambda i: (0, 0, 0)
    row_spec = pl.BlockSpec((block, hidden), lambda i: (i, 0))
    return pl.pallas_call(
        mlp_kernel,
        grid=(total // block,),
        out_shape=jax.ShapeDtypeStruct(rows.shape, BF16),
        in_specs=[row_spec, pl.BlockSpec((1, hidden, ff), whole), pl.BlockSpec((1, hidden, ff), whole), pl.BlockSpec((1, ff, hidden), whole)],
        out_specs=row_spec,
        compiler_params=params(),
        cost_estimate=cost(6 * total * hidden * ff, 4 * total * hidden + 6 * hidden * ff),
        name="mlp",
    )(rows, w_gate, w_up, w_down)


def combine(gates, pos, rows, resid, slots, block):
    total, hidden = rows.shape
    tokens, experts = pos.shape
    return pl.pallas_call(
        functools.partial(combine_kernel, slots),
        grid=(total // block,),
        out_shape=jax.ShapeDtypeStruct((tokens, hidden), BF16),
        in_specs=[
            pl.BlockSpec((3, tokens, experts), lambda i: (0, 0, 0)),
            pl.BlockSpec((tokens, experts), lambda i: (0, 0)),
            pl.BlockSpec((block, hidden), lambda i: (i, 0)),
            pl.BlockSpec((tokens, hidden), lambda i: (0, 0)),
        ],
        out_specs=pl.BlockSpec((tokens, hidden), lambda i: (0, 0)),
        scratch_shapes=[pltpu.VMEM((tokens, hidden), F32)],
        compiler_params=params(),
        cost_estimate=cost(6 * tokens * total * hidden, 2 * total * hidden),
        name="combine",
    )(gates, pos, rows, resid)


def solution(mesh):
    def local_block(x_in, norm_gain, w_router, expert_ids, w_gate, w_up, w_down):
        tokens, hidden = x_in.shape
        experts = w_router.shape[1]
        h, gates, pos, pos_t = route(x_in, norm_gain, w_router, expert_ids)
        outgoing = pack(h, pos_t, SLOTS, 16)
        received = exchange(outgoing, experts)
        y = mlp(received, w_gate, w_up, w_down, 512)
        returned = exchange(y, experts)
        return combine(gates, pos, returned, x_in, SLOTS, 512)

    tok_spec = P(("dp", "ep"), None)
    expert_spec = P("ep", None, None)
    return jax.shard_map(local_block, mesh=mesh, in_specs=(tok_spec, P(None), P(None, None), tok_spec, expert_spec, expert_spec, expert_spec), out_specs=tok_spec, check_vma=False)
```

time: 904 us -> 562 us (0.62)
  the two profiles are of different devices: /device:TPU:2 before, /device:TPU:31 now
where the time goes in v1:
time: 562 us; the launch traced here: 561 us
  blocking collectives  478 us (85%)
  Pallas kernels  80.2 us (14%)
    all_to_all x2, blocking collectives, exchange(): return lax.all_to_all(blocks, 'ep', 0, 0, tiled=True).reshape(rows.shape)  478 us
    pallas_call x1, Pallas kernels, mlp(): pl.pallas_call(mlp_kernel, grid=(total // block,), out_shape=jax.ShapeDty...  46.2 us
    pallas_call x1, Pallas kernels, combine(): pl.pallas_call(functools.partial(combine_kernel, slots), grid=(total // b...  20.4 us

profile of v1, /device:TPU:31, one launch (start us, length us, event | category | flops | bytes accessed | tf_op | source)
XLA Modules:
  0.0 561.1 jit_solution(11236526920258925073)
XLA Ops:
  0.0 1.3 reshape.15.gain_ref
  1.3 1.5 copy.8.ids_ref
  2.8 3.3 route.1
  6.1 10.2 %pack.1 = bf16[4096,2048]{1,0:T(8,128)(2,1)} custom-call(bf16[256,2048]{1,0:T(8,128)(2,1)} %get-tuple-element.11.h_ref, f32[128,256]{1,0:T(8,128)} %get-tuple-element.12.post_ref), custom_call_target="tpu_custom_call" | custom-call | flops 4294967296 | bytes 16777216 | tf_op jit(solution)/shard_map/pack/pallas_call | solution.py:120
  16.3 240.9 %all_to_all.10 = bf16[128,32,2048]{2,1,0:T(8,128)(2,1)} all-to-all(bf16[128,32,2048]{2,1,0:T(8,128)(2,1)} %bitcast.5), channel_id=1, replica_groups=mesh['dp'=1,'ep'=128] {'ep'}, dimensions={0} | all-to-all | bytes 33554432 | tf_op jit(solution)/shard_map/all_to_all | solution.py:134
  257.2 46.2 %mlp.1 = bf16[4096,2048]{1,0:T(8,128)(2,1)} custom-call(bf16[4096,2048]{1,0:T(8,128)(2,1)} %bitcast.7, bf16[1,2048,768]{2,1,0:T(8,128)(2,1)} %wg_ref.1, bf16[1,2048,768]{2,1,0:T(8,128)(2,1)} %wu_ref.1, bf16[1,768,2048]{2,1,0:T(8,128)(2,1)} %wd_ref.1), custom_call_target="tpu_custom_call" | custom-call | flops 38654705664 | bytes 42991616 | tf_op jit(solution)/shard_map/mlp/pallas_call | solution.py:142
  303.4 237.2 %all_to_all.11 = bf16[128,32,2048]{2,1,0:T(8,128)(2,1)} all-to-all(bf16[128,32,2048]{2,1,0:T(8,128)(2,1)} %bitcast.8), channel_id=1, replica_groups=mesh['dp'=1,'ep'=128] {'ep'}, dimensions={0} | all-to-all | bytes 33554432 | tf_op jit(solution)/shard_map/all_to_all | solution.py:134
  540.7 20.4 %combine.1 = bf16[256,2048]{1,0:T(8,128)(2,1)} custom-call(bf16[3,256,128]{2,1,0:T(8,128)(2,1)} %get-tuple-element.9.gate_ref, bf16[256,128]{1,0:T(8,128)(2,1)} %get-tuple-element.10.pos_ref, bf16[4096,2048]{1,0:T(8,128)(2,1)} %bitcast.6, bf16[256,2048]{1,0:T(8,128)(2,1)} %base_ref.1), custom_call_target="tpu_custom_call" | custom-call | flops 12884901888 | bytes 16777216 | tf_op jit(solution)/shard_map/combine/pallas_call | solution.py:157

commit v2 on v0

v2 whole, which is shorter than its diff:
```python
import functools

import jax
import jax.numpy as jnp
from jax import lax
from jax.experimental import pallas as pl
from jax.experimental.pallas import tpu as pltpu
from jax.sharding import PartitionSpec as P

EPS = 1e-6
SLOTS = 32
SIDE = 4
STRIDES = (2, 8, 32)
WIDTHS = (768, 640, 640)
STARTS = (0, 768, 1408)
PLANE = 32
F32, BF16, I32 = jnp.float32, jnp.bfloat16, jnp.int32
MESH = pl.DeviceIdType.MESH


def shifted(dev, axis, step):
    stride = STRIDES[axis]
    here = lax.rem(lax.div(dev, stride), SIDE)
    return dev + (lax.rem(here + step, SIDE) - here) * stride


def plane_axes(axis):
    return tuple(a for a in (2, 1, 0) if a != axis)


def in_plane(dev, axis, p):
    a, b = plane_axes(axis)
    dev = shifted(shifted(dev, a, lax.div(p, 8)), b, lax.rem(lax.div(p, 2), SIDE))
    core = lax.rem(dev, 2)
    return dev + lax.rem(core + lax.rem(p, 2), 2) - core


def opposite(p):
    da, db = lax.div(p, 8), lax.rem(lax.div(p, 2), SIDE)
    return lax.rem(SIDE - da, SIDE) * 8 + lax.rem(SIDE - db, SIDE) * 2 + lax.rem(p, 2)


def relative(axis, along, p):
    a, b = plane_axes(axis)
    place = {axis: along, a: lax.div(p, 8), b: lax.rem(lax.div(p, 2), SIDE)}
    return (place[2] * SIDE + place[1]) * 8 + place[0] * 2 + lax.rem(p, 2)


def split_relative(axis, rho):
    place = (lax.rem(lax.div(rho, 2), SIDE), lax.rem(lax.div(rho, 8), SIDE), lax.div(rho, 32))
    a, b = plane_axes(axis)
    return place[axis], place[a] * 8 + place[b] * 2 + lax.rem(rho, 2)


def remote(src, dst, send_sem, recv_sem, dev):
    return pltpu.make_async_remote_copy(src, dst, send_sem, recv_sem, device_id={"ep": dev}, device_id_type=MESH)


def wait_for(ref, sem):
    pltpu.make_async_copy(ref, ref, sem).wait()


def source(axis, r):
    return 0 if r == 0 else 3 * axis + r


def route_kernel(x_ref, gain_ref, wr_ref, ids_ref, idst_ref, h_ref, gate_ref):
    tokens, experts = x_ref.shape[0], wr_ref.shape[1]
    top_k = ids_ref.shape[1]
    resid = x_ref[...].astype(F32)
    mean_sq = jnp.mean(resid * resid, axis=-1, keepdims=True)
    normed = (resid * lax.rsqrt(mean_sq + EPS) * gain_ref[...].astype(F32)).astype(BF16)
    h_ref[...] = normed
    logits = jnp.dot(normed, wr_ref[...], preferred_element_type=F32)
    exps = jnp.exp(logits - jnp.max(logits, axis=-1, keepdims=True))
    router_p = exps / jnp.sum(exps, axis=-1, keepdims=True)
    lane_expert = lax.broadcasted_iota(I32, (tokens, experts), 1)
    chosen = jnp.zeros((tokens, experts), F32)
    for j in range(top_k):
        chosen += jnp.where(ids_ref[:, j:j + 1] == lane_expert, 1.0, 0.0)
    picked = router_p * chosen
    gates_t = jnp.transpose(picked / jnp.sum(picked, axis=-1, keepdims=True))
    row_expert = lax.broadcasted_iota(I32, (experts, tokens), 0)
    for j in range(top_k):
        gate_ref[j:j + 1, :] = jnp.sum(jnp.where(idst_ref[j:j + 1, :] == row_expert, gates_t, 0.0), axis=0, keepdims=True)


def dispatch_kernel(h_ref, ids_ref, gate_ref, post_ref, gates_ref, recv0, recv1, recv2,
                    line0, line1, line2, ids_scr, gate_scr, pack0, pack1, pack2,
                    line_send, line_recv, ids_send, ids_recv, gate_send, gate_recv, send_sem, recv_sem, local_sem):
    recv, line, pack = (recv0, recv1, recv2), (line0, line1, line2), (pack0, pack1, pack2)
    top_k, tokens = ids_ref.shape
    experts = post_ref.shape[1]
    me = lax.axis_index("ep")
    for r in (1, 3, 2):
        for axis in range(3):
            dev, k = shifted(me, axis, r), source(axis, SIDE - r)
            n = k - 1
            remote(ids_ref, ids_scr.at[n], ids_send, ids_recv.at[n], dev).start()
            remote(gate_ref, gate_scr.at[n], gate_send, gate_recv.at[n], dev).start()
            cols = h_ref.at[:, pl.ds(STARTS[axis], WIDTHS[axis])]
            remote(cols, line[axis].at[SIDE - r - 1], line_send.at[axis], line_recv.at[n], dev).start()

    row_expert = lax.broadcasted_iota(I32, (experts, tokens), 0)
    rows = lax.broadcasted_iota(I32, (tokens, tokens), 0)
    upper = jnp.where(rows < lax.broadcasted_iota(I32, (tokens, tokens), 1), 1.0, 0.0).astype(BF16)
    slot = lax.broadcasted_iota(I32, (SLOTS, tokens), 0).astype(F32)

    def tables(k, ids, gates):
        chosen = jnp.zeros((experts, tokens), F32)
        dense = jnp.zeros((experts, tokens), F32)
        for j in range(top_k):
            hit = ids[j:j + 1, :] == row_expert
            chosen += jnp.where(hit, 1.0, 0.0)
            dense += jnp.where(hit, gates[j:j + 1, :], 0.0)
        before = jnp.dot(chosen.astype(BF16), upper, preferred_element_type=F32)
        post_ref[k] = jnp.where(chosen > 0.0, before, 255.0)
        gates_ref[k] = dense

    for r in (0, 1, 3, 2):
        for axis in range(3):
            k = source(axis, r)
            if r == 0 and axis == 0:
                tables(0, ids_ref[...], gate_ref[...])
            elif r > 0:
                wait_for(ids_scr.at[k - 1], ids_recv.at[k - 1])
                wait_for(gate_scr.at[k - 1], gate_recv.at[k - 1])
                tables(k, ids_scr[k - 1], gate_scr[k - 1])
                wait_for(line[axis].at[r - 1], line_recv.at[k - 1])

        def chunk(q, carry, r=r):
            for axis in range(3):
                k = source(axis, r)
                picks = []
                for j in range(8):
                    expert = in_plane(me, axis, q * 8 + j)
                    picks.append(jnp.where(post_ref[k, pl.ds(expert, 1), :] == slot, 1.0, 0.0).astype(BF16))
                if r == 0:
                    own = h_ref[:, STARTS[axis]:STARTS[axis] + WIDTHS[axis]]
                else:
                    own = line[axis][r - 1]
                packed = jnp.dot(jnp.concatenate(picks, axis=0), own, preferred_element_type=F32).astype(BF16)
                pack[axis][pl.ds((r * 4 + q) * 8, 8)] = packed.reshape(8, SLOTS, WIDTHS[axis])

            def send(j, c):
                p = q * 8 + j
                for axis in range(3):
                    src = pack[axis].at[r * PLANE + p]
                    dst = recv[axis].at[relative(axis, r, opposite(p))]

                    @pl.when(p == 0)
                    def _():
                        pltpu.make_async_copy(src, dst, local_sem.at[axis, r]).start()

                    @pl.when(p != 0)
                    def _():
                        remote(src, dst, send_sem.at[axis], recv_sem.at[axis], in_plane(me, axis, p)).start()
                return c

            lax.fori_loop(0, 8, send, 0)
            return carry

        lax.fori_loop(0, 4, chunk, 0)

    wait_for(ids_scr, ids_send)
    wait_for(gate_scr, gate_send)
    far = SIDE * (PLANE - 1)
    for axis in range(3):
        wait_for(line[axis], line_send.at[axis])
        for r in range(SIDE):
            wait_for(recv[axis].at[0], local_sem.at[axis, r])
        wait_for(pack[axis].at[pl.ds(0, far)], send_sem.at[axis])
        wait_for(recv[axis].at[pl.ds(0, far)], recv_sem.at[axis])


def expert_kernel(block, x0, x1, x2, wg_ref, wu_ref, wd_ref, ret0, ret1, ret2,
                  in0, in1, in2, out0, out1, out2, load_sem, send_sem, recv_sem, local_sem):
    x, ret, held, done = (x0, x1, x2), (ret0, ret1, ret2), (in0, in1, in2), (out0, out1, out2)
    me = lax.axis_index("ep")
    blocks = x0.shape[0] // block

    def load(b, axis):
        part = pl.ds(b * block, block)
        return pltpu.make_async_copy(x[axis].at[part], held[axis].at[part], load_sem.at[axis, b])

    for b in range(blocks):
        for axis in range(3):
            load(b, axis).start()

    def step(b, carry):
        for axis in range(3):
            load(b, axis).wait()
        gate_val, up_val = 0.0, 0.0
        for axis in range(3):
            rows = held[axis][pl.ds(b * block, block)].reshape(block * SLOTS, WIDTHS[axis])
            span = slice(STARTS[axis], STARTS[axis] + WIDTHS[axis])
            gate_val += jnp.dot(rows, wg_ref[0, span, :], preferred_element_type=F32)
            up_val += jnp.dot(rows, wu_ref[0, span, :], preferred_element_type=F32)
        act = (jax.nn.silu(gate_val) * up_val).astype(BF16)
        for axis in range(3):
            span = slice(STARTS[axis], STARTS[axis] + WIDTHS[axis])
            y = jnp.dot(act, wd_ref[0, :, span], preferred_element_type=F32).astype(BF16)
            done[axis][pl.ds(b * block, block)] = y.reshape(block, SLOTS, WIDTHS[axis])

        def send(j, c):
            rho = b * block + j
            for axis in range(3):
                along, p = split_relative(axis, rho)
                src = done[axis].at[rho]
                dst = ret[axis].at[along * PLANE + opposite(p)]

                @pl.when(p == 0)
                def _():
                    pltpu.make_async_copy(src, dst, local_sem.at[axis, along]).start()

                @pl.when(p != 0)
                def _():
                    remote(src, dst, send_sem.at[axis], recv_sem.at[axis], in_plane(me, axis, p)).start()
            return c

        lax.fori_loop(0, block, send, 0)
        return carry

    lax.fori_loop(0, blocks, step, 0)
    far = SIDE * (PLANE - 1)
    for axis in range(3):
        for r in range(SIDE):
            wait_for(ret[axis].at[0], local_sem.at[axis, r])
        wait_for(done[axis].at[pl.ds(0, far)], send_sem.at[axis])
        wait_for(ret[axis].at[pl.ds(0, far)], recv_sem.at[axis])


def combine_kernel(x_ref, post_ref, gates_ref, y0, y1, y2, out_ref,
                   in0, in1, in2, sum0, sum1, sum2, part0, part1, part2, load_sem, send_sem, recv_sem):
    y, held, sums, parts = (y0, y1, y2), (in0, in1, in2), (sum0, sum1, sum2), (part0, part1, part2)
    tokens = x_ref.shape[0]
    experts = post_ref.shape[1]
    me = lax.axis_index("ep")
    half = PLANE // 2
    width = half * SLOTS
    order = (1, 3, 2, 0)

    def load(axis, r):
        part = pl.ds(r * PLANE, PLANE)
        return pltpu.make_async_copy(y[axis].at[part], held[axis].at[part], load_sem.at[axis, r])

    for r in order:
        for axis in range(3):
            load(axis, r).start()

    expert = lax.broadcasted_iota(I32, (experts, width), 0)
    column = lax.broadcasted_iota(I32, (experts, width), 1)
    slot = (lax.broadcasted_iota(I32, (tokens, width), 1) % SLOTS).astype(F32)

    def copy(axis, r):
        return remote(sums[axis].at[r], parts[axis].at[SIDE - r - 1], send_sem.at[axis, r - 1], recv_sem.at[axis, SIDE - r - 1], shifted(me, axis, r))

    for r in order:
        for axis in range(3):
            k = source(axis, r)
            gates = jnp.transpose(gates_ref[k])
            high = gates.astype(BF16)
            rest = gates - high.astype(F32)
            mid = rest.astype(BF16)
            low = (rest - mid.astype(F32)).astype(BF16)
            table = jnp.concatenate([high, mid, low, jnp.transpose(post_ref[k]).astype(BF16)], axis=0)
            load(axis, r).wait()

            def chunk(c, carry, r=r, axis=axis, table=table):
                spread = jnp.where(in_plane(me, axis, column // SLOTS + c * half) == expert, 1.0, 0.0).astype(BF16)
                wide = jnp.dot(table, spread, preferred_element_type=F32)
                hit = wide[3 * tokens:] == slot
                weight = jnp.concatenate([jnp.where(hit, wide[i * tokens:(i + 1) * tokens], 0.0).astype(BF16) for i in range(3)], axis=0)
                rows = held[axis][pl.ds(r * PLANE + c * half, half)].reshape(width, WIDTHS[axis])
                got = jnp.dot(weight, rows, preferred_element_type=F32)
                total = got[:tokens] + got[tokens:2 * tokens] + got[2 * tokens:]

                @pl.when(c == 0)
                def _():
                    sums[axis][r] = total

                @pl.when(c != 0)
                def _():
                    sums[axis][r] += total
                return carry

            lax.fori_loop(0, 2, chunk, 0)
        if r > 0:
            for axis in range(3):
                copy(axis, r).start()

    for axis in range(3):
        span = slice(STARTS[axis], STARTS[axis] + WIDTHS[axis])
        total = x_ref[:, span].astype(F32) + sums[axis][0]
        for r in range(1, SIDE):
            wait_for(parts[axis].at[r - 1], recv_sem.at[axis, r - 1])
            total += parts[axis][r - 1]
        out_ref[:, span] = total.astype(out_ref.dtype)
    for axis in range(3):
        for r in range(1, SIDE):
            wait_for(sums[axis].at[r], send_sem.at[axis, r - 1])


def params(**kw):
    return pltpu.CompilerParams(vmem_limit_bytes=62 * 2 ** 20, **kw)


VMEM = pl.BlockSpec(memory_space=pltpu.VMEM)
ANY = pl.BlockSpec(memory_space=pl.ANY)
DMA = pltpu.SemaphoreType.DMA
shape = jax.ShapeDtypeStruct


def route(x_in, norm_gain, w_router, expert_ids):
    tokens, hidden = x_in.shape
    top_k = expert_ids.shape[1]
    return pl.pallas_call(
        route_kernel,
        out_shape=(shape((tokens, hidden), BF16), shape((top_k, tokens), F32)),
        compiler_params=params(),
        name="route",
    )(x_in, norm_gain.reshape(1, hidden), w_router, expert_ids, expert_ids.T)


def dispatch(h, ids_t, gates, devices):
    top_k, tokens = ids_t.shape
    table = shape((10, devices, tokens), F32)
    return pl.pallas_call(
        dispatch_kernel,
        out_shape=(table, table) + tuple(shape((devices, SLOTS, w), BF16) for w in WIDTHS),
        in_specs=[VMEM] * 3,
        out_specs=(VMEM, VMEM, ANY, ANY, ANY),
        scratch_shapes=[pltpu.VMEM((3, tokens, w), BF16) for w in WIDTHS]
        + [pltpu.VMEM((9, top_k, tokens), I32), pltpu.VMEM((9, top_k, tokens), F32)]
        + [pltpu.VMEM((devices, SLOTS, w), BF16) for w in WIDTHS]
        + [DMA((3,)), DMA((9,)), DMA, DMA((9,)), DMA, DMA((9,)), DMA((3,)), DMA((3,)), DMA((3, SIDE))],
        compiler_params=params(has_side_effects=True),
        name="dispatch",
    )(h, ids_t, gates)


def experts_mlp(rows, w_gate, w_up, w_down, block):
    devices = rows[0].shape[0]
    blocks = [pltpu.VMEM((devices, SLOTS, w), BF16) for w in WIDTHS]
    return pl.pallas_call(
        functools.partial(expert_kernel, block),
        out_shape=tuple(shape(r.shape, BF16) for r in rows),
        in_specs=[ANY] * 3 + [VMEM] * 3,
        out_specs=(ANY,) * 3,
        scratch_shapes=blocks + blocks + [DMA((3, devices // block)), DMA((3,)), DMA((3,)), DMA((3, SIDE))],
        compiler_params=params(has_side_effects=True),
        name="experts",
    )(*rows, w_gate, w_up, w_down)


def combine(x_in, post, gates, rows):
    tokens, hidden = x_in.shape
    devices = rows[0].shape[0]
    return pl.pallas_call(
        combine_kernel,
        out_shape=shape((tokens, hidden), BF16),
        in_specs=[VMEM] * 3 + [ANY] * 3,
        out_specs=VMEM,
        scratch_shapes=[pltpu.VMEM((devices, SLOTS, w), BF16) for w in WIDTHS]
        + [pltpu.VMEM((SIDE, tokens, w), F32) for w in WIDTHS]
        + [pltpu.VMEM((3, tokens, w), F32) for w in WIDTHS]
        + [DMA((3, SIDE)), DMA((3, 3)), DMA((3, 3))],
        compiler_params=params(has_side_effects=True),
        name="combine",
    )(x_in, post, gates, *rows)


def solution(mesh):
    def local_block(x_in, norm_gain, w_router, expert_ids, w_gate, w_up, w_down):
        h, gates = route(x_in, norm_gain, w_router, expert_ids)
        post, dense, *rows = dispatch(h, expert_ids.T, gates, w_router.shape[1])
        returned = experts_mlp(rows, w_gate, w_up, w_down, 16)
        return combine(x_in, post, dense, returned)

    tok_spec = P(("dp", "ep"), None)
    expert_spec = P("ep", None, None)
    return jax.shard_map(local_block, mesh=mesh, in_specs=(tok_spec, P(None), P(None, None), tok_spec, expert_spec, expert_spec, expert_spec), out_specs=tok_spec, check_vma=False)
```

time: 904 us -> 474 us (0.52)
  Pallas kernels: 0 us -> 469 us
  local copies, waits for them, and re-layouts: 249 us -> 5.06 us
  waiting for transfers between devices: 231 us -> 0 us
  blocking collectives: 224 us -> 0 us
  other arithmetic: 128 us -> 0 us
  matrix products: 53.3 us -> 0 us
  starting transfers between devices: 14.8 us -> 0 us
    pallas_call x0 -> x4, Pallas kernels: none -> 469 us  [the longest x1 220 us: experts_mlp(): pl.pallas_call(functools.partial(expert_kernel, block), out_shape=tuple((...]
    all_to_all x1 -> x0, waiting for transfers between devices: 231 us -> none  [local_block(): lax.all_to_all(outputs, 'ep', 1, 0, tiled=True)]
    all_to_all x1 -> x0, blocking collectives: 224 us -> none  [local_block(): received = lax.all_to_all(outgoing, 'ep', 0, 1, tiled=True)]
    unnamed x29 -> x2, local copies, waits for them, and re-layouts: 136 us -> 3.78 us
    unnamed x1 -> x0, other arithmetic: 99.6 us -> none
    gather x7 -> x0, local copies, waits for them, and re-layouts: 74.3 us -> none  [the longest x1 32.7 us: local_block(): jnp.take(normed, slot_tok, axis=0, mode='fill', fill_value=0)]
    dot_general x3 -> x0, matrix products: 53.3 us -> none  [the longest x1 36.5 us: expert_mlp(): jnp.einsum('erf,efd->erd', hidden_act, w_down, preferred_element_type=jnp...]
    convert_element_type x1 -> x0, local copies, waits for them, and re-layouts: 29.2 us -> none  [expert_mlp(): jnp.einsum('erf,efd->erd', hidden_act, w_down, preferred_element_type=jnp...]
  transfers between devices with their start and end apart: 1 -> 0, of which waited for: 1 -> 0; matrix products, arithmetic and copies ran while one was open for 2% -> 0% of each run, Pallas kernels for 0% -> 0%
where the time goes in v2:
time: 474 us
  Pallas kernels  469 us (99%)
  local copies, waits for them, and re-layouts  5.06 us (1%)
    pallas_call x1, Pallas kernels, experts_mlp(): pl.pallas_call(functools.partial(expert_kernel, block), out_shape=tuple((...  220 us
    pallas_call x1, Pallas kernels, dispatch(): pl.pallas_call(dispatch_kernel, out_shape=(table, table) + tuple((shape((...  178 us
    pallas_call x1, Pallas kernels, combine(): pl.pallas_call(combine_kernel, out_shape=shape((tokens, hidden), BF16), i...  68 us

profile of v2, /device:TPU:2, one launch (start us, length us, event | category | flops | bytes accessed | tf_op | source)
XLA Modules:
  0.0 473.9 jit_solution(5159847746994718234)
XLA Ops:
  0.0 1.3 reshape.3.gain_ref
  1.3 1.5 copy.8.ids_ref
  2.8 3.2 route.1
  6.0 177.7 %dispatch.1 = (f32[10,128,256]{2,1,0:T(8,128)}, f32[10,128,256]{2,1,0:T(8,128)}, bf16[128,32,768]{2,1,0:T(8,128)(2,1)}, bf16[128,32,640]{2,1,0:T(8,128)(2,1)}, bf16[128,32,640]{2,1,0:T(8,128)(2,1)}) custom-call(bf16[256,2048]{1,0:T(8,128)(2,1)} %get-tuple-element.15.h_ref, s32[8,256]{1,0:T(8,128)} %bitcast.2, f32[8,256]{1,0:T(8,128)} %get-tuple-element.16.gate_ref), custom_call_target="tpu_custom_call" | custom-call | tf_op jit(solution)/shard_map/dispatch/pallas_call | solution.py:328
  183.7 219.9 %experts.1 = (bf16[128,32,768]{2,1,0:T(8,128)(2,1)}, bf16[128,32,640]{2,1,0:T(8,128)(2,1)}, bf16[128,32,640]{2,1,0:T(8,128)(2,1)}) custom-call(bf16[128,32,768]{2,1,0:T(8,128)(2,1)} %get-tuple-element.19.x0, bf16[128,32,640]{2,1,0:T(8,128)(2,1)} %get-tuple-element.20.x1, bf16[128,32,640]{2,1,0:T(8,128)(2,1)} %get-tuple-element.21.x2, ...), custom_call_target="tpu_custom_call" | custom-call | tf_op jit(solution)/shard_map/experts/pallas_call | solution.py:345
  403.6 68.0 %combine.1 = bf16[256,2048]{1,0:T(8,128)(2,1)} custom-call(bf16[256,2048]{1,0:T(8,128)(2,1)} %x_ref.3, f32[10,128,256]{2,1,0:T(8,128)} %get-tuple-element.17.post_ref, f32[10,128,256]{2,1,0:T(8,128)} %get-tuple-element.18.gates_ref, bf16[128,32,768]{2,1,0:T(8,128)(2,1)} %get-tuple-element.22.y0, bf16[128,32,640]{2,1,0:T(8,128)(2,1)} %get-tuple-element.23.y1, ...), custom_call_target="tpu_custom_call" | custom-call | tf_op jit(solution)/shard_map/combine/pallas_call | solution.py:359
  471.6 2.3 copy.10

commit v3 on v2

v3 whole, which is shorter than its diff:
```python
import functools

import jax
import jax.numpy as jnp
from jax import lax
from jax.experimental import pallas as pl
from jax.experimental.pallas import tpu as pltpu
from jax.sharding import PartitionSpec as P

EPS = 1e-6
SLOTS = 32
SIDE = 4
STRIDES = (2, 8, 32)
WIDTHS = (768, 640, 640)
STARTS = (0, 768, 1408)
PLANE = 32
LAG = 2
F32, BF16, I32 = jnp.float32, jnp.bfloat16, jnp.int32
MESH = pl.DeviceIdType.MESH


def shifted(dev, axis, step):
    stride = STRIDES[axis]
    here = lax.rem(lax.div(dev, stride), SIDE)
    return dev + (lax.rem(here + step, SIDE) - here) * stride


def plane_axes(axis):
    return tuple(a for a in (2, 1, 0) if a != axis)


def in_plane(dev, axis, p):
    a, b = plane_axes(axis)
    dev = shifted(shifted(dev, a, lax.div(p, 8)), b, lax.rem(lax.div(p, 2), SIDE))
    core = lax.rem(dev, 2)
    return dev + lax.rem(core + lax.rem(p, 2), 2) - core


def opposite(p):
    da, db = lax.div(p, 8), lax.rem(lax.div(p, 2), SIDE)
    return lax.rem(SIDE - da, SIDE) * 8 + lax.rem(SIDE - db, SIDE) * 2 + lax.rem(p, 2)


def bit(block, axis):
    return lax.rem(lax.div(block, 1 << axis), 2)


def member(axis, block, m):
    a, b = plane_axes(axis)
    return (bit(block, a) + 2 * lax.div(m, 4)) * 8 + (bit(block, b) + 2 * lax.rem(lax.div(m, 2), 2)) * 2 + lax.rem(m, 2)


def place_of(axis, along, p):
    a, b = plane_axes(axis)
    step = {axis: along, a: lax.div(p, 8), b: lax.rem(lax.div(p, 2), SIDE)}
    odd = (lax.rem(step[2], 2) * 2 + lax.rem(step[1], 2)) * 2 + lax.rem(step[0], 2)
    half = (lax.div(step[2], 2) * 2 + lax.div(step[1], 2)) * 2 + lax.div(step[0], 2)
    return odd * 16 + half * 2 + lax.rem(p, 2)


def split_place(axis, place):
    block, half = lax.div(place, 16), lax.div(lax.rem(place, 16), 2)
    step = tuple(bit(block, i) + 2 * bit(half, i) for i in range(3))
    a, b = plane_axes(axis)
    return step[axis], step[a] * 8 + step[b] * 2 + lax.rem(place, 2)


def remote(src, dst, send_sem, recv_sem, dev):
    return pltpu.make_async_remote_copy(src, dst, send_sem, recv_sem, device_id={"ep": dev}, device_id_type=MESH)


def wait_for(ref, sem):
    pltpu.make_async_copy(ref, ref, sem).wait()


def source(axis, r):
    return 0 if r == 0 else 3 * axis + r


def place_in_tables(axis, r):
    return (3 * axis + r) * lax.min(r, 1)


def route_kernel(x_ref, gain_ref, wr_ref, ids_ref, idst_ref, h_ref, gate_ref):
    tokens, experts = x_ref.shape[0], wr_ref.shape[1]
    top_k = ids_ref.shape[1]
    resid = x_ref[...].astype(F32)
    mean_sq = jnp.mean(resid * resid, axis=-1, keepdims=True)
    normed = (resid * lax.rsqrt(mean_sq + EPS) * gain_ref[...].astype(F32)).astype(BF16)
    h_ref[...] = normed
    logits = jnp.dot(normed, wr_ref[...], preferred_element_type=F32)
    exps = jnp.exp(logits - jnp.max(logits, axis=-1, keepdims=True))
    router_p = exps / jnp.sum(exps, axis=-1, keepdims=True)
    lane_expert = lax.broadcasted_iota(I32, (tokens, experts), 1)
    chosen = jnp.zeros((tokens, experts), F32)
    for j in range(top_k):
        chosen += jnp.where(ids_ref[:, j:j + 1] == lane_expert, 1.0, 0.0)
    picked = router_p * chosen
    gates_t = jnp.transpose(picked / jnp.sum(picked, axis=-1, keepdims=True))
    row_expert = lax.broadcasted_iota(I32, (experts, tokens), 0)
    for j in range(top_k):
        gate_ref[j:j + 1, :] = jnp.sum(jnp.where(idst_ref[j:j + 1, :] == row_expert, gates_t, 0.0), axis=0, keepdims=True)


def dispatch_kernel(h_ref, ids_ref, gate_ref, post_ref, gates_ref, recv0, recv1, recv2,
                    line0, line1, line2, ids_scr, gate_scr, pack0, pack1, pack2,
                    line_send, line_recv, ids_send, ids_recv, gate_send, gate_recv, send_sem, recv_sem, local_sem):
    recv, line, pack = (recv0, recv1, recv2), (line0, line1, line2), (pack0, pack1, pack2)
    top_k, tokens = ids_ref.shape
    experts = post_ref.shape[1]
    me = lax.axis_index("ep")
    for r in (2, 1, 3):
        for axis in range(3):
            dev, k = shifted(me, axis, r), source(axis, SIDE - r)
            n = k - 1
            remote(ids_ref, ids_scr.at[n], ids_send, ids_recv.at[n], dev).start()
            remote(gate_ref, gate_scr.at[n], gate_send, gate_recv.at[n], dev).start()
            cols = h_ref.at[:, pl.ds(STARTS[axis], WIDTHS[axis])]
            remote(cols, line[axis].at[SIDE - r], line_send.at[axis], line_recv.at[n], dev).start()

    row_expert = lax.broadcasted_iota(I32, (experts, tokens), 0)
    rows = lax.broadcasted_iota(I32, (tokens, tokens), 0)
    upper = jnp.where(rows < lax.broadcasted_iota(I32, (tokens, tokens), 1), 1.0, 0.0).astype(BF16)
    slot = lax.broadcasted_iota(I32, (SLOTS, tokens), 0).astype(F32)

    def tables(k, ids, gates):
        chosen = jnp.zeros((experts, tokens), F32)
        dense = jnp.zeros((experts, tokens), F32)
        for j in range(top_k):
            hit = ids[j:j + 1, :] == row_expert
            chosen += jnp.where(hit, 1.0, 0.0)
            dense += jnp.where(hit, gates[j:j + 1, :], 0.0)
        before = jnp.dot(chosen.astype(BF16), upper, preferred_element_type=F32)
        post_ref[k] = jnp.where(chosen > 0.0, before, 255.0)
        gates_ref[k] = dense

    tables(0, ids_ref[...], gate_ref[...])
    for axis in range(3):
        line[axis][0] = h_ref[:, STARTS[axis]:STARTS[axis] + WIDTHS[axis]]

    def arrive(axis, r):
        n = source(axis, r) - 1
        wait_for(ids_scr.at[n], ids_recv.at[n])
        wait_for(gate_scr.at[n], gate_recv.at[n])
        tables(n + 1, ids_scr[n], gate_scr[n])
        wait_for(line[axis].at[r], line_recv.at[n])

    def step(n, carry):
        b, two = lax.div(n, 2), lax.rem(n, 2)
        for axis in range(3):
            @pl.when(n == 1)
            def _():
                arrive(axis, 2)

            @pl.when(n == (2 << axis))
            def _():
                arrive(axis, 1)

            @pl.when(n == (2 << axis) + 1)
            def _():
                arrive(axis, 3)

            r = bit(b, axis) + 2 * two
            k = place_in_tables(axis, r)
            picks = []
            for m in range(8):
                expert = in_plane(me, axis, member(axis, b, m))
                picks.append(jnp.where(post_ref[k, pl.ds(expert, 1), :] == slot, 1.0, 0.0).astype(BF16))
            packed = jnp.dot(jnp.concatenate(picks, axis=0), line[axis][r], preferred_element_type=F32).astype(BF16)
            pack[axis][pl.ds(n * 8, 8)] = packed.reshape(8, SLOTS, WIDTHS[axis])

        def send(m, c):
            for axis in range(3):
                r = bit(b, axis) + 2 * two
                p = member(axis, b, m)
                src = pack[axis].at[n * 8 + m]
                dst = recv[axis].at[place_of(axis, r, opposite(p))]

                @pl.when(p == 0)
                def _():
                    pltpu.make_async_copy(src, dst, local_sem.at[axis, r]).start()

                @pl.when(p != 0)
                def _():
                    remote(src, dst, send_sem.at[axis], recv_sem.at[axis], in_plane(me, axis, p)).start()
            return c

        lax.fori_loop(0, 8, send, 0)
        return carry

    lax.fori_loop(0, 16, step, 0)
    wait_for(ids_scr, ids_send)
    wait_for(gate_scr, gate_send)
    far = SIDE * (PLANE - 1)
    for axis in range(3):
        wait_for(line[axis].at[pl.ds(1, 3)], line_send.at[axis])
        for r in range(SIDE):
            wait_for(recv[axis].at[0], local_sem.at[axis, r])
        wait_for(pack[axis].at[pl.ds(0, far)], send_sem.at[axis])
        wait_for(recv[axis].at[pl.ds(0, far)], recv_sem.at[axis])


def expert_kernel(x_ref, post_ref, gates_ref, x0, x1, x2, wg_ref, wu_ref, wd_ref, out_ref, ret0, ret1, ret2,
                  row0, row1, row2, in0, in1, in2, sum0, sum1, sum2, part0, part1, part2, table_ref,
                  load_sem, back_sem, send_sem, recv_sem, local_sem, line_send, line_recv):
    x, ret, rows, held = (x0, x1, x2), (ret0, ret1, ret2), (row0, row1, row2), (in0, in1, in2)
    sums, parts = (sum0, sum1, sum2), (part0, part1, part2)
    me = lax.axis_index("ep")
    tokens, experts = x_ref.shape[0], post_ref.shape[1]
    blocks, size, width = 8, 16, 8 * SLOTS

    def load(b, axis):
        part = pl.ds(b * size, size)
        return pltpu.make_async_copy(x[axis].at[part], rows[axis].at[part], load_sem.at[axis, b])

    for b in range(blocks):
        for axis in range(3):
            load(b, axis).start()
    for axis in range(3):
        sums[axis][...] = jnp.zeros(sums[axis].shape, F32)

    def mlp(b):
        for axis in range(3):
            load(b, axis).wait()
        gate_val, up_val = 0.0, 0.0
        for axis in range(3):
            part = rows[axis][pl.ds(b * size, size)].reshape(size * SLOTS, WIDTHS[axis])
            span = slice(STARTS[axis], STARTS[axis] + WIDTHS[axis])
            gate_val += jnp.dot(part, wg_ref[0, span, :], preferred_element_type=F32)
            up_val += jnp.dot(part, wu_ref[0, span, :], preferred_element_type=F32)
        act = (jax.nn.silu(gate_val) * up_val).astype(BF16)
        for axis in range(3):
            span = slice(STARTS[axis], STARTS[axis] + WIDTHS[axis])
            y = jnp.dot(act, wd_ref[0, :, span], preferred_element_type=F32).astype(BF16)
            rows[axis][pl.ds(b * size, size)] = y.reshape(size, SLOTS, WIDTHS[axis])

        def send(j, c):
            place = b * size + j
            for axis in range(3):
                along, p = split_place(axis, place)
                src, dst = rows[axis].at[place], ret[axis].at[place]

                @pl.when(p == 0)
                def _():
                    pltpu.make_async_copy(src, dst, local_sem.at[axis, along]).start()

                @pl.when(p != 0)
                def _():
                    remote(src, dst, send_sem.at[axis], recv_sem.at[axis, b], in_plane(me, axis, p)).start()
            return c

        lax.fori_loop(0, size, send, 0)

    def fill_tables(k, c):
        gates = jnp.transpose(gates_ref[k])
        high = gates.astype(BF16)
        rest = gates - high.astype(F32)
        mid = rest.astype(BF16)
        low = (rest - mid.astype(F32)).astype(BF16)
        table_ref[k] = jnp.concatenate([high, mid, low, jnp.transpose(post_ref[k]).astype(BF16)], axis=0)
        return c

    def partial(axis, r):
        return remote(sums[axis].at[r], parts[axis].at[SIDE - r - 1], line_send.at[axis, r - 1], line_recv.at[axis, SIDE - r - 1], shifted(me, axis, r))

    expert = lax.broadcasted_iota(I32, (experts, width), 0)
    column = lax.div(lax.broadcasted_iota(I32, (1, width), 1), SLOTS)
    slot = lax.rem(lax.broadcasted_iota(I32, (1, width), 1), SLOTS).astype(F32)

    def back(b, axis):
        return pltpu.make_async_copy(ret[axis].at[pl.ds(b * size, size)], held[axis], back_sem.at[axis])

    def gather(b):
        for axis in range(3):
            a1, a2 = plane_axes(axis)
            odd = bit(b, axis)
            near = bit(b, a1) + bit(b, a2) == 0

            @pl.when(near)
            def _():
                wait_for(ret[axis].at[0], local_sem.at[axis, odd])
                wait_for(ret[axis].at[0], local_sem.at[axis, odd + 2])
                wait_for(ret[axis].at[pl.ds(0, size - 2)], recv_sem.at[axis, b])

            @pl.when(jnp.logical_not(near))
            def _():
                wait_for(ret[axis].at[pl.ds(0, size)], recv_sem.at[axis, b])

            back(b, axis).start()
        for axis in range(3):
            back(b, axis).wait()
            theirs = in_plane(me, axis, opposite(member(axis, b, column)))
            spread = jnp.where(theirs == expert, 1.0, 0.0).astype(BF16)
            for two in range(2):
                r = bit(b, axis) + 2 * two
                wide = jnp.dot(table_ref[place_in_tables(axis, r)], spread, preferred_element_type=F32)
                hit = wide[3 * tokens:] == slot
                weight = jnp.concatenate([jnp.where(hit, wide[i * tokens:(i + 1) * tokens], 0.0).astype(BF16) for i in range(3)], axis=0)
                run = 2 << axis
                pieces = [held[axis][i:i + run].reshape(run * SLOTS, WIDTHS[axis]) for i in range(two * run, size, 2 * run)]
                got = jnp.dot(weight, jnp.concatenate(pieces, axis=0), preferred_element_type=F32)
                sums[axis][r] += got[:tokens] + got[tokens:2 * tokens] + got[2 * tokens:]
        for axis in range(3):
            @pl.when(b == 7 - (1 << axis))
            def _():
                partial(axis, 2).start()

    def step(t, carry):
        @pl.when(t < blocks)
        def _():
            mlp(t)

        @pl.when(t == LAG - 1)
        def _():
            lax.fori_loop(0, table_ref.shape[0], fill_tables, 0)

        @pl.when(t >= LAG)
        def _():
            gather(t - LAG)
        return carry

    lax.fori_loop(0, blocks + LAG, step, 0)
    for axis in range(3):
        for r in (1, 3):
            partial(axis, r).start()
    for axis in range(3):
        span = slice(STARTS[axis], STARTS[axis] + WIDTHS[axis])
        total = x_ref[:, span].astype(F32) + sums[axis][0]
        for r in (2, 1, 3):
            wait_for(parts[axis].at[r - 1], line_recv.at[axis, r - 1])
            total += parts[axis][r - 1]
        out_ref[:, span] = total.astype(out_ref.dtype)
    far = SIDE * (PLANE - 1)
    for axis in range(3):
        for r in range(1, SIDE):
            wait_for(sums[axis].at[r], line_send.at[axis, r - 1])
        wait_for(rows[axis].at[pl.ds(0, far)], send_sem.at[axis])


def params(**kw):
    return pltpu.CompilerParams(vmem_limit_bytes=62 * 2 ** 20, **kw)


VMEM = pl.BlockSpec(memory_space=pltpu.VMEM)
ANY = pl.BlockSpec(memory_space=pl.ANY)
DMA = pltpu.SemaphoreType.DMA
shape = jax.ShapeDtypeStruct


def route(x_in, norm_gain, w_router, expert_ids):
    tokens, hidden = x_in.shape
    top_k = expert_ids.shape[1]
    return pl.pallas_call(
        route_kernel,
        out_shape=(shape((tokens, hidden), BF16), shape((top_k, tokens), F32)),
        compiler_params=params(),
        name="route",
    )(x_in, norm_gain.reshape(1, hidden), w_router, expert_ids, expert_ids.T)


def dispatch(h, ids_t, gates, devices):
    top_k, tokens = ids_t.shape
    table = shape((10, devices, tokens), F32)
    return pl.pallas_call(
        dispatch_kernel,
        out_shape=(table, table) + tuple(shape((devices, SLOTS, w), BF16) for w in WIDTHS),
        in_specs=[VMEM] * 3,
        out_specs=(VMEM, VMEM, ANY, ANY, ANY),
        scratch_shapes=[pltpu.VMEM((SIDE, tokens, w), BF16) for w in WIDTHS]
        + [pltpu.VMEM((9, top_k, tokens), I32), pltpu.VMEM((9, top_k, tokens), F32)]
        + [pltpu.VMEM((devices, SLOTS, w), BF16) for w in WIDTHS]
        + [DMA((3,)), DMA((9,)), DMA, DMA((9,)), DMA, DMA((9,)), DMA((3,)), DMA((3,)), DMA((3, SIDE))],
        compiler_params=params(has_side_effects=True),
        name="dispatch",
    )(h, ids_t, gates)


def experts_mlp(x_in, post, gates, rows, w_gate, w_up, w_down):
    tokens, hidden = x_in.shape
    devices = rows[0].shape[0]
    out, *_ = pl.pallas_call(
        expert_kernel,
        out_shape=(shape((tokens, hidden), BF16),) + tuple(shape(r.shape, BF16) for r in rows),
        in_specs=[VMEM] * 3 + [ANY] * 3 + [VMEM] * 3,
        out_specs=(VMEM,) + (ANY,) * 3,
        scratch_shapes=[pltpu.VMEM((devices, SLOTS, w), BF16) for w in WIDTHS]
        + [pltpu.VMEM((16, SLOTS, w), BF16) for w in WIDTHS]
        + [pltpu.VMEM((SIDE, tokens, w), F32) for w in WIDTHS]
        + [pltpu.VMEM((3, tokens, w), F32) for w in WIDTHS]
        + [pltpu.VMEM((10, 4 * tokens, devices), BF16)]
        + [DMA((3, 8)), DMA((3,)), DMA((3,)), DMA((3, 8)), DMA((3, SIDE)), DMA((3, 3)), DMA((3, 3))],
        compiler_params=params(has_side_effects=True),
        name="experts",
    )(x_in, post, gates, *rows, w_gate, w_up, w_down)
    return out


def solution(mesh):
    def local_block(x_in, norm_gain, w_router, expert_ids, w_gate, w_up, w_down):
        h, gates = route(x_in, norm_gain, w_router, expert_ids)
        post, dense, *rows = dispatch(h, expert_ids.T, gates, w_router.shape[1])
        return experts_mlp(x_in, post, dense, rows, w_gate, w_up, w_down)

    tok_spec = P(("dp", "ep"), None)
    expert_spec = P("ep", None, None)
    return jax.shard_map(local_block, mesh=mesh, in_specs=(tok_spec, P(None), P(None, None), tok_spec, expert_spec, expert_spec, expert_spec), out_specs=tok_spec, check_vma=False)
```

time: 474 us -> 405 us (0.85); the launches traced: 474 us -> 400 us
  Pallas kernels: 469 us -> 395 us
    pallas_call x2 -> x1, Pallas kernels: 288 us -> 217 us  [experts_mlp(): pl.pallas_call(expert_kernel, out_shape=(shape((tokens, hidden), BF16),)...]
where the time goes in v3:
time: 405 us; the launch traced here: 400 us
  Pallas kernels  395 us (98%)
  local copies, waits for them, and re-layouts  5.06 us (1%)
    pallas_call x1, Pallas kernels, experts_mlp(): pl.pallas_call(expert_kernel, out_shape=(shape((tokens, hidden), BF16),)...  217 us
    pallas_call x1, Pallas kernels, dispatch(): pl.pallas_call(dispatch_kernel, out_shape=(table, table) + tuple((shape((...  174 us

profile of v3, /device:TPU:2, one launch (start us, length us, event | category | flops | bytes accessed | tf_op | source)
XLA Modules:
  0.0 400.1 jit_solution(9310579118660720398)
XLA Ops:
  0.0 1.3 reshape.3.gain_ref
  1.3 1.5 copy.8.ids_ref
  2.8 3.2 route.1
  6.0 174.5 %dispatch.1 = (f32[10,128,256]{2,1,0:T(8,128)}, f32[10,128,256]{2,1,0:T(8,128)}, bf16[128,32,768]{2,1,0:T(8,128)(2,1)}, bf16[128,32,640]{2,1,0:T(8,128)(2,1)}, bf16[128,32,640]{2,1,0:T(8,128)(2,1)}) custom-call(bf16[256,2048]{1,0:T(8,128)(2,1)} %get-tuple-element.13.h_ref, s32[8,256]{1,0:T(8,128)} %bitcast.2, f32[8,256]{1,0:T(8,128)} %get-tuple-element.14.gate_ref), custom_call_target="tpu_custom_call" | custom-call | tf_op jit(solution)/shard_map/dispatch/pallas_call | solution.py:364
  180.5 217.3 %experts.1 = (bf16[256,2048]{1,0:T(8,128)(2,1)}, bf16[128,32,768]{2,1,0:T(8,128)(2,1)}, bf16[128,32,640]{2,1,0:T(8,128)(2,1)}, bf16[128,32,640]{2,1,0:T(8,128)(2,1)}) custom-call(bf16[256,2048]{1,0:T(8,128)(2,1)} %x_ref.3, f32[10,128,256]{2,1,0:T(8,128)} %get-tuple-element.15.post_ref, f32[10,128,256]{2,1,0:T(8,128)} %get-tuple-element.16.gates_ref, ...), custom_call_target="tpu_custom_call" | custom-call | tf_op jit(solution)/shard_map/experts/pallas_call | solution.py:381
  397.8 2.3 copy.10

commit v4 on v3

--- a/solution.py
+++ b/solution.py
@@ -14,7 +14,7 @@
 WIDTHS = (768, 640, 640)
 STARTS = (0, 768, 1408)
 PLANE = 32
-LAG = 2
+LAG = 4
 F32, BF16, I32 = jnp.float32, jnp.bfloat16, jnp.int32
 MESH = pl.DeviceIdType.MESH
 
@@ -50,12 +50,10 @@
     return (bit(block, a) + 2 * lax.div(m, 4)) * 8 + (bit(block, b) + 2 * lax.rem(lax.div(m, 2), 2)) * 2 + lax.rem(m, 2)
 
 
-def place_of(axis, along, p):
-    a, b = plane_axes(axis)
-    step = {axis: along, a: lax.div(p, 8), b: lax.rem(lax.div(p, 2), SIDE)}
+def place_of(step, core):
     odd = (lax.rem(step[2], 2) * 2 + lax.rem(step[1], 2)) * 2 + lax.rem(step[0], 2)
     half = (lax.div(step[2], 2) * 2 + lax.div(step[1], 2)) * 2 + lax.div(step[0], 2)
-    return odd * 16 + half * 2 + lax.rem(p, 2)
+    return odd * 16 + half * 2 + core
 
 
 def split_place(axis, place):
@@ -109,19 +107,93 @@
     top_k, tokens = ids_ref.shape
     experts = post_ref.shape[1]
     me = lax.axis_index("ep")
+
+    def forward(axis, r, src):
+        for q in (2, 1, 3):
+            n = r * SIDE + SIDE - q
+            remote(src, line[axis].at[n], line_send.at[axis], line_recv.at[axis, n], shifted(me, (axis + 1) % 3, q)).start()
+
+    for axis in range(3):
+        for n in range(1, SIDE * SIDE):
+            r, q = n // SIDE, n % SIDE
+            dev = shifted(shifted(me, axis, r), (axis + 1) % 3, q)
+            there = ((SIDE - r) % SIDE) * SIDE + (SIDE - q) % SIDE
+            remote(ids_ref, ids_scr.at[axis, there], ids_send.at[axis], ids_recv.at[axis], dev).start()
     for r in (2, 1, 3):
         for axis in range(3):
-            dev, k = shifted(me, axis, r), source(axis, SIDE - r)
-            n = k - 1
-            remote(ids_ref, ids_scr.at[n], ids_send, ids_recv.at[n], dev).start()
-            remote(gate_ref, gate_scr.at[n], gate_send, gate_recv.at[n], dev).start()
-            cols = h_ref.at[:, pl.ds(STARTS[axis], WIDTHS[axis])]
-            remote(cols, line[axis].at[SIDE - r], line_send.at[axis], line_recv.at[n], dev).start()
+            n = (SIDE - r) * SIDE
+            src = h_ref.at[:, pl.ds(STARTS[axis], WIDTHS[axis])]
+            remote(src, line[axis].at[n], line_send.at[axis], line_recv.at[axis, n], shifted(me, axis, r)).start()
+    for axis in range(3):
+        forward(axis, 0, h_ref.at[:, pl.ds(STARTS[axis], WIDTHS[axis])])
+    for axis in range(3):
+        for r in range(1, SIDE):
+            k = 3 * axis + SIDE - r - 1
+            remote(gate_ref, gate_scr.at[k], gate_send, gate_recv, shifted(me, axis, r)).start()
+        line[axis][0] = h_ref[:, STARTS[axis]:STARTS[axis] + WIDTHS[axis]]
+        ids_scr[axis, 0] = ids_ref[...]
 
     row_expert = lax.broadcasted_iota(I32, (experts, tokens), 0)
     rows = lax.broadcasted_iota(I32, (tokens, tokens), 0)
     upper = jnp.where(rows < lax.broadcasted_iota(I32, (tokens, tokens), 1), 1.0, 0.0).astype(BF16)
-    slot = lax.broadcasted_iota(I32, (SLOTS, tokens), 0).astype(F32)
+    slot = lax.broadcasted_iota(I32, (8, SLOTS, tokens), 1).astype(F32)
+    eight = lax.broadcasted_iota(I32, (8, tokens), 0)
+
+    def across(axis, m):
+        dev = shifted(me, (axis + 2) % 3, lax.div(m, 2))
+        core = lax.rem(dev, 2)
+        return dev + lax.rem(core + lax.rem(m, 2), 2) - core
+
+    def swap(v):
+        return v + lax.div(v, 2) * (5 - 2 * v)
+
+    def step(t, carry):
+        r, q = swap(lax.rem(t, SIDE)), swap(lax.div(t, SIDE))
+        n = r * SIDE + q
+        for axis in range(3):
+            @pl.when(t == 1)
+            def _():
+                wait_for(ids_scr.at[axis, pl.ds(1, SIDE * SIDE - 1)], ids_recv.at[axis])
+
+            @pl.when(t > 0)
+            def _():
+                wait_for(line[axis].at[n], line_recv.at[axis, n])
+
+            @pl.when((t > 0) & (t < SIDE))
+            def _():
+                forward(axis, r, line[axis].at[n])
+
+            theirs = across(axis, eight)
+            chosen = jnp.zeros((8, tokens), F32)
+            for j in range(top_k):
+                chosen += jnp.where(ids_scr[axis, n, j:j + 1, :] == theirs, 1.0, 0.0)
+            before = jnp.dot(chosen.astype(BF16), upper, preferred_element_type=F32)
+            post = jnp.where(chosen > 0.0, before, 255.0)
+            pick = jnp.where(post[:, None, :] == slot, 1.0, 0.0).astype(BF16).reshape(8 * SLOTS, tokens)
+            packed = jnp.dot(pick, line[axis][n], preferred_element_type=F32).astype(BF16)
+            pack[axis][pl.ds(t * 8, 8)] = packed.reshape(8, SLOTS, WIDTHS[axis])
+
+        def send(i, c):
+            m = lax.rem(i + 2, 8)
+            for axis in range(3):
+                steps = {axis: r, (axis + 1) % 3: q, (axis + 2) % 3: lax.rem(SIDE - lax.div(m, 2), SIDE)}
+                src = pack[axis].at[t * 8 + m]
+                dst = recv[axis].at[place_of(steps, lax.rem(m, 2))]
+
+                @pl.when(m == 0)
+                def _():
+                    pltpu.make_async_copy(src, dst, local_sem.at[axis, t]).start()
+
+                @pl.when(m != 0)
+                def _():
+                    remote(src, dst, send_sem.at[axis], recv_sem.at[axis], across(axis, m)).start()
+            return c
+
+        lax.fori_loop(0, 8, send, 0)
+        return carry
+
+    steps = SIDE * SIDE
+    lax.fori_loop(0, steps, step, 0)
 
     def tables(k, ids, gates):
         chosen = jnp.zeros((experts, tokens), F32)
@@ -134,70 +206,21 @@
         post_ref[k] = jnp.where(chosen > 0.0, before, 255.0)
         gates_ref[k] = dense
 
+    wait_for(gate_scr, gate_recv)
     tables(0, ids_ref[...], gate_ref[...])
     for axis in range(3):
-        line[axis][0] = h_ref[:, STARTS[axis]:STARTS[axis] + WIDTHS[axis]]
-
-    def arrive(axis, r):
-        n = source(axis, r) - 1
-        wait_for(ids_scr.at[n], ids_recv.at[n])
-        wait_for(gate_scr.at[n], gate_recv.at[n])
-        tables(n + 1, ids_scr[n], gate_scr[n])
-        wait_for(line[axis].at[r], line_recv.at[n])
-
-    def step(n, carry):
-        b, two = lax.div(n, 2), lax.rem(n, 2)
-        for axis in range(3):
-            @pl.when(n == 1)
-            def _():
-                arrive(axis, 2)
-
-            @pl.when(n == (2 << axis))
-            def _():
-                arrive(axis, 1)
-
-            @pl.when(n == (2 << axis) + 1)
-            def _():
-                arrive(axis, 3)
-
-            r = bit(b, axis) + 2 * two
-            k = place_in_tables(axis, r)
-            picks = []
-            for m in range(8):
-                expert = in_plane(me, axis, member(axis, b, m))
-                picks.append(jnp.where(post_ref[k, pl.ds(expert, 1), :] == slot, 1.0, 0.0).astype(BF16))
-            packed = jnp.dot(jnp.concatenate(picks, axis=0), line[axis][r], preferred_element_type=F32).astype(BF16)
-            pack[axis][pl.ds(n * 8, 8)] = packed.reshape(8, SLOTS, WIDTHS[axis])
-
-        def send(m, c):
-            for axis in range(3):
-                r = bit(b, axis) + 2 * two
-                p = member(axis, b, m)
-                src = pack[axis].at[n * 8 + m]
-                dst = recv[axis].at[place_of(axis, r, opposite(p))]
-
-                @pl.when(p == 0)
-                def _():
-                    pltpu.make_async_copy(src, dst, local_sem.at[axis, r]).start()
-
-                @pl.when(p != 0)
-                def _():
-                    remote(src, dst, send_sem.at[axis], recv_sem.at[axis], in_plane(me, axis, p)).start()
-            return c
-
-        lax.fori_loop(0, 8, send, 0)
-        return carry
-
-    lax.fori_loop(0, 16, step, 0)
-    wait_for(ids_scr, ids_send)
+        for r in range(1, SIDE):
+            k = source(axis, r)
+            tables(k, ids_scr[axis, r * SIDE], gate_scr[k - 1])
+
     wait_for(gate_scr, gate_send)
-    far = SIDE * (PLANE - 1)
-    for axis in range(3):
-        wait_for(line[axis].at[pl.ds(1, 3)], line_send.at[axis])
-        for r in range(SIDE):
-            wait_for(recv[axis].at[0], local_sem.at[axis, r])
-        wait_for(pack[axis].at[pl.ds(0, far)], send_sem.at[axis])
-        wait_for(recv[axis].at[pl.ds(0, far)], recv_sem.at[axis])
+    for axis in range(3):
+        wait_for(ids_scr.at[axis, pl.ds(1, steps - 1)], ids_send.at[axis])
+        wait_for(line[axis].at[pl.ds(1, steps - 1)], line_send.at[axis])
+        for t in range(steps):
+            wait_for(recv[axis].at[0], local_sem.at[axis, t])
+        wait_for(pack[axis].at[pl.ds(0, 7 * steps)], send_sem.at[axis])
+        wait_for(recv[axis].at[pl.ds(0, 7 * steps)], recv_sem.at[axis])
 
 
 def expert_kernel(x_ref, post_ref, gates_ref, x0, x1, x2, wg_ref, wu_ref, wd_ref, out_ref, ret0, ret1, ret2,
@@ -366,10 +389,10 @@
         out_shape=(table, table) + tuple(shape((devices, SLOTS, w), BF16) for w in WIDTHS),
         in_specs=[VMEM] * 3,
         out_specs=(VMEM, VMEM, ANY, ANY, ANY),
-        scratch_shapes=[pltpu.VMEM((SIDE, tokens, w), BF16) for w in WIDTHS]
-        + [pltpu.VMEM((9, top_k, tokens), I32), pltpu.VMEM((9, top_k, tokens), F32)]
+        scratch_shapes=[pltpu.VMEM((SIDE * SIDE, tokens, w), BF16) for w in WIDTHS]
+        + [pltpu.VMEM((3, SIDE * SIDE, top_k, tokens), I32), pltpu.VMEM((9, top_k, tokens), F32)]
         + [pltpu.VMEM((devices, SLOTS, w), BF16) for w in WIDTHS]
-        + [DMA((3,)), DMA((9,)), DMA, DMA((9,)), DMA, DMA((9,)), DMA((3,)), DMA((3,)), DMA((3, SIDE))],
+        + [DMA((3,)), DMA((3, SIDE * SIDE)), DMA((3,)), DMA((3,)), DMA, DMA, DMA((3,)), DMA((3,)), DMA((3, SIDE * SIDE))],
         compiler_params=params(has_side_effects=True),
         name="dispatch",
     )(h, ids_t, gates)

time: 405 us -> 379 us (0.936)
  Pallas kernels: 395 us -> 368 us
    pallas_call x1, Pallas kernels: 174 us -> 159 us  [dispatch(): pl.pallas_call(dispatch_kernel, out_shape=(table, table) + tuple((shape((...]
    pallas_call x1, Pallas kernels: 217 us -> 206 us  [experts_mlp(): pl.pallas_call(expert_kernel, out_shape=(shape((tokens, hidden), BF16),)...]
where the time goes in v4:
time: 379 us; the launch traced here: 373 us
  Pallas kernels  368 us (97%)
  local copies, waits for them, and re-layouts  5.06 us (1%)
    pallas_call x1, Pallas kernels, experts_mlp(): pl.pallas_call(expert_kernel, out_shape=(shape((tokens, hidden), BF16),)...  206 us
    pallas_call x1, Pallas kernels, dispatch(): pl.pallas_call(dispatch_kernel, out_shape=(table, table) + tuple((shape((...  159 us

profile of v4, /device:TPU:2, one launch (start us, length us, event | category | flops | bytes accessed | tf_op | source)
XLA Modules:
  0.0 373.4 jit_solution(7403794791995001414)
XLA Ops:
  0.0 1.3 reshape.3.gain_ref
  1.3 1.5 copy.8.ids_ref
  2.8 3.2 route.1
  6.0 159.2 %dispatch.1 = (f32[10,128,256]{2,1,0:T(8,128)}, f32[10,128,256]{2,1,0:T(8,128)}, bf16[128,32,768]{2,1,0:T(8,128)(2,1)}, bf16[128,32,640]{2,1,0:T(8,128)(2,1)}, bf16[128,32,640]{2,1,0:T(8,128)(2,1)}) custom-call(bf16[256,2048]{1,0:T(8,128)(2,1)} %get-tuple-element.13.h_ref, s32[8,256]{1,0:T(8,128)} %bitcast.2, f32[8,256]{1,0:T(8,128)} %get-tuple-element.14.gate_ref), custom_call_target="tpu_custom_call" | custom-call | tf_op jit(solution)/shard_map/dispatch/pallas_call | solution.py:387
  165.2 206.0 %experts.1 = (bf16[256,2048]{1,0:T(8,128)(2,1)}, bf16[128,32,768]{2,1,0:T(8,128)(2,1)}, bf16[128,32,640]{2,1,0:T(8,128)(2,1)}, bf16[128,32,640]{2,1,0:T(8,128)(2,1)}) custom-call(bf16[256,2048]{1,0:T(8,128)(2,1)} %x_ref.3, f32[10,128,256]{2,1,0:T(8,128)} %get-tuple-element.15.post_ref, f32[10,128,256]{2,1,0:T(8,128)} %get-tuple-element.16.gates_ref, ...), custom_call_target="tpu_custom_call" | custom-call | tf_op jit(solution)/shard_map/experts/pallas_call | solution.py:404
  371.1 2.3 copy.10

commit v5 on v4

--- a/solution.py
+++ b/solution.py
@@ -13,8 +13,9 @@
 STRIDES = (2, 8, 32)
 WIDTHS = (768, 640, 640)
 STARTS = (0, 768, 1408)
+CUT = 384
 PLANE = 32
-LAG = 4
+LAG = 7
 F32, BF16, I32 = jnp.float32, jnp.bfloat16, jnp.int32
 MESH = pl.DeviceIdType.MESH
 
@@ -109,9 +110,13 @@
     me = lax.axis_index("ep")
 
     def forward(axis, r, src):
-        for q in (2, 1, 3):
+        for q in (1, 3):
             n = r * SIDE + SIDE - q
             remote(src, line[axis].at[n], line_send.at[axis], line_recv.at[axis, n], shifted(me, (axis + 1) % 3, q)).start()
+
+    def pass_on(axis, r, q, first):
+        part, n = pl.ds(first, tokens // 2), r * SIDE + 2
+        remote(line[axis].at[r * SIDE + q, part], line[axis].at[n, part], line_send.at[axis], line_recv.at[axis, n], shifted(me, (axis + 1) % 3, SIDE - q)).start()
 
     for axis in range(3):
         for n in range(1, SIDE * SIDE):
@@ -162,6 +167,14 @@
             @pl.when((t > 0) & (t < SIDE))
             def _():
                 forward(axis, r, line[axis].at[n])
+
+            @pl.when((t >= SIDE) & (t < 2 * SIDE))
+            def _():
+                pass_on(axis, r, 1, tokens // 2)
+
+            @pl.when((t >= 2 * SIDE) & (t < 3 * SIDE))
+            def _():
+                pass_on(axis, r, 3, 0)
 
             theirs = across(axis, eight)
             chosen = jnp.zeros((8, tokens), F32)
@@ -224,13 +237,14 @@
 
 
 def expert_kernel(x_ref, post_ref, gates_ref, x0, x1, x2, wg_ref, wu_ref, wd_ref, out_ref, ret0, ret1, ret2,
-                  row0, row1, row2, in0, in1, in2, sum0, sum1, sum2, part0, part1, part2, table_ref,
+                  row0, row1, row2, in0, in1, in2, sum0, sum1, sum2, part0, part1, part2, act_ref, table_ref,
                   load_sem, back_sem, send_sem, recv_sem, local_sem, line_send, line_recv):
     x, ret, rows, held = (x0, x1, x2), (ret0, ret1, ret2), (row0, row1, row2), (in0, in1, in2)
     sums, parts = (sum0, sum1, sum2), (part0, part1, part2)
     me = lax.axis_index("ep")
     tokens, experts = x_ref.shape[0], post_ref.shape[1]
     blocks, size, width = 8, 16, 8 * SLOTS
+    spans = [[pl.ds(0, CUT) for w in WIDTHS], [pl.ds(CUT, w - CUT) for w in WIDTHS]]
 
     def load(b, axis):
         part = pl.ds(b * size, size)
@@ -242,7 +256,7 @@
     for axis in range(3):
         sums[axis][...] = jnp.zeros(sums[axis].shape, F32)
 
-    def mlp(b):
+    def activate(b):
         for axis in range(3):
             load(b, axis).wait()
         gate_val, up_val = 0.0, 0.0
@@ -251,25 +265,27 @@
             span = slice(STARTS[axis], STARTS[axis] + WIDTHS[axis])
             gate_val += jnp.dot(part, wg_ref[0, span, :], preferred_element_type=F32)
             up_val += jnp.dot(part, wu_ref[0, span, :], preferred_element_type=F32)
-        act = (jax.nn.silu(gate_val) * up_val).astype(BF16)
-        for axis in range(3):
-            span = slice(STARTS[axis], STARTS[axis] + WIDTHS[axis])
-            y = jnp.dot(act, wd_ref[0, :, span], preferred_element_type=F32).astype(BF16)
-            rows[axis][pl.ds(b * size, size)] = y.reshape(size, SLOTS, WIDTHS[axis])
+        act_ref[b] = (jax.nn.silu(gate_val) * up_val).astype(BF16)
+
+    def project(b, turn):
+        for axis in range(3):
+            span = spans[turn][axis]
+            y = jnp.dot(act_ref[b], wd_ref[0, :, pl.ds(STARTS[axis] + span.start, span.size)], preferred_element_type=F32).astype(BF16)
+            rows[axis][pl.ds(b * size, size), :, span] = y.reshape(size, SLOTS, span.size)
 
         def send(j, c):
             place = b * size + j
             for axis in range(3):
                 along, p = split_place(axis, place)
-                src, dst = rows[axis].at[place], ret[axis].at[place]
+                src, dst = rows[axis].at[place, :, spans[turn][axis]], ret[axis].at[place, :, spans[turn][axis]]
 
                 @pl.when(p == 0)
                 def _():
-                    pltpu.make_async_copy(src, dst, local_sem.at[axis, along]).start()
+                    pltpu.make_async_copy(src, dst, local_sem.at[axis, turn * SIDE + along]).start()
 
                 @pl.when(p != 0)
                 def _():
-                    remote(src, dst, send_sem.at[axis], recv_sem.at[axis, b], in_plane(me, axis, p)).start()
+                    remote(src, dst, send_sem.at[axis, turn], recv_sem.at[axis, turn * blocks + b], in_plane(me, axis, p)).start()
             return c
 
         lax.fori_loop(0, size, send, 0)
@@ -283,35 +299,38 @@
         table_ref[k] = jnp.concatenate([high, mid, low, jnp.transpose(post_ref[k]).astype(BF16)], axis=0)
         return c
 
-    def partial(axis, r):
-        return remote(sums[axis].at[r], parts[axis].at[SIDE - r - 1], line_send.at[axis, r - 1], line_recv.at[axis, SIDE - r - 1], shifted(me, axis, r))
+    def partial(axis, r, turn):
+        span = spans[turn][axis]
+        return remote(sums[axis].at[r, :, span], parts[axis].at[SIDE - r - 1, :, span], line_send.at[axis, turn * 3 + r - 1], line_recv.at[axis, turn * 3 + SIDE - r - 1], shifted(me, axis, r))
 
     expert = lax.broadcasted_iota(I32, (experts, width), 0)
     column = lax.div(lax.broadcasted_iota(I32, (1, width), 1), SLOTS)
     slot = lax.rem(lax.broadcasted_iota(I32, (1, width), 1), SLOTS).astype(F32)
 
-    def back(b, axis):
-        return pltpu.make_async_copy(ret[axis].at[pl.ds(b * size, size)], held[axis], back_sem.at[axis])
-
-    def gather(b):
+    def gather(b, turn):
+        def back(axis):
+            span = spans[turn][axis]
+            return pltpu.make_async_copy(ret[axis].at[pl.ds(b * size, size), :, span], held[axis].at[:, :, span], back_sem.at[axis])
+
         for axis in range(3):
             a1, a2 = plane_axes(axis)
-            odd = bit(b, axis)
+            odd, span = bit(b, axis), spans[turn][axis]
             near = bit(b, a1) + bit(b, a2) == 0
 
             @pl.when(near)
             def _():
-                wait_for(ret[axis].at[0], local_sem.at[axis, odd])
-                wait_for(ret[axis].at[0], local_sem.at[axis, odd + 2])
-                wait_for(ret[axis].at[pl.ds(0, size - 2)], recv_sem.at[axis, b])
+                wait_for(ret[axis].at[0, :, span], local_sem.at[axis, turn * SIDE + odd])
+                wait_for(ret[axis].at[0, :, span], local_sem.at[axis, turn * SIDE + odd + 2])
+                wait_for(ret[axis].at[pl.ds(0, size - 2), :, span], recv_sem.at[axis, turn * blocks + b])
 
             @pl.when(jnp.logical_not(near))
             def _():
-                wait_for(ret[axis].at[pl.ds(0, size)], recv_sem.at[axis, b])
-
-            back(b, axis).start()
-        for axis in range(3):
-            back(b, axis).wait()
+                wait_for(ret[axis].at[pl.ds(0, size), :, span], recv_sem.at[axis, turn * blocks + b])
+
+            back(axis).start()
+        for axis in range(3):
+            span = spans[turn][axis]
+            back(axis).wait()
             theirs = in_plane(me, axis, opposite(member(axis, b, column)))
             spread = jnp.where(theirs == expert, 1.0, 0.0).astype(BF16)
             for two in range(2):
@@ -320,44 +339,59 @@
                 hit = wide[3 * tokens:] == slot
                 weight = jnp.concatenate([jnp.where(hit, wide[i * tokens:(i + 1) * tokens], 0.0).astype(BF16) for i in range(3)], axis=0)
                 run = 2 << axis
-                pieces = [held[axis][i:i + run].reshape(run * SLOTS, WIDTHS[axis]) for i in range(two * run, size, 2 * run)]
+                pieces = [held[axis][i:i + run, :, span].reshape(run * SLOTS, span.size) for i in range(two * run, size, 2 * run)]
                 got = jnp.dot(weight, jnp.concatenate(pieces, axis=0), preferred_element_type=F32)
-                sums[axis][r] += got[:tokens] + got[tokens:2 * tokens] + got[2 * tokens:]
+                sums[axis][r, :, span] += got[:tokens] + got[tokens:2 * tokens] + got[2 * tokens:]
         for axis in range(3):
             @pl.when(b == 7 - (1 << axis))
             def _():
-                partial(axis, 2).start()
+                partial(axis, 2, turn).start()
+
+            @pl.when(b == 7)
+            def _():
+                partial(axis, 1, turn).start()
+                partial(axis, 3, turn).start()
 
     def step(t, carry):
         @pl.when(t < blocks)
         def _():
-            mlp(t)
+            activate(t)
+            project(t, 0)
+
+        @pl.when((t >= blocks) & (t < 2 * blocks))
+        def _():
+            project(t - blocks, 1)
 
         @pl.when(t == LAG - 1)
         def _():
             lax.fori_loop(0, table_ref.shape[0], fill_tables, 0)
 
-        @pl.when(t >= LAG)
+        @pl.when((t >= LAG) & (t < blocks + LAG))
         def _():
-            gather(t - LAG)
+            gather(t - LAG, 0)
+
+        @pl.when(t >= blocks + LAG)
+        def _():
+            gather(t - blocks - LAG, 1)
         return carry
 
-    lax.fori_loop(0, blocks + LAG, step, 0)
-    for axis in range(3):
-        for r in (1, 3):
-            partial(axis, r).start()
-    for axis in range(3):
-        span = slice(STARTS[axis], STARTS[axis] + WIDTHS[axis])
-        total = x_ref[:, span].astype(F32) + sums[axis][0]
-        for r in (2, 1, 3):
-            wait_for(parts[axis].at[r - 1], line_recv.at[axis, r - 1])
-            total += parts[axis][r - 1]
-        out_ref[:, span] = total.astype(out_ref.dtype)
+    lax.fori_loop(0, 2 * blocks + LAG, step, 0)
     far = SIDE * (PLANE - 1)
-    for axis in range(3):
-        for r in range(1, SIDE):
-            wait_for(sums[axis].at[r], line_send.at[axis, r - 1])
-        wait_for(rows[axis].at[pl.ds(0, far)], send_sem.at[axis])
+    for turn in range(2):
+        for axis in range(3):
+            span = spans[turn][axis]
+            cols = slice(STARTS[axis] + span.start, STARTS[axis] + span.start + span.size)
+            total = x_ref[:, cols].astype(F32) + sums[axis][0, :, span]
+            for r in (2, 1, 3):
+                wait_for(parts[axis].at[r - 1, :, span], line_recv.at[axis, turn * 3 + r - 1])
+                total += parts[axis][r - 1, :, span]
+            out_ref[:, cols] = total.astype(out_ref.dtype)
+    for turn in range(2):
+        for axis in range(3):
+            span = spans[turn][axis]
+            for r in range(1, SIDE):
+                wait_for(sums[axis].at[r, :, span], line_send.at[axis, turn * 3 + r - 1])
+            wait_for(rows[axis].at[pl.ds(0, far), :, span], send_sem.at[axis, turn])
 
 
 def params(**kw):
@@ -410,8 +444,8 @@
         + [pltpu.VMEM((16, SLOTS, w), BF16) for w in WIDTHS]
         + [pltpu.VMEM((SIDE, tokens, w), F32) for w in WIDTHS]
         + [pltpu.VMEM((3, tokens, w), F32) for w in WIDTHS]
-        + [pltpu.VMEM((10, 4 * tokens, devices), BF16)]
-        + [DMA((3, 8)), DMA((3,)), DMA((3,)), DMA((3, 8)), DMA((3, SIDE)), DMA((3, 3)), DMA((3, 3))],
+        + [pltpu.VMEM((8, 16 * SLOTS, w_gate.shape[2]), BF16), pltpu.VMEM((10, 4 * tokens, devices), BF16)]
+        + [DMA((3, 8)), DMA((3,)), DMA((3, 2)), DMA((3, 16)), DMA((3, 2 * SIDE)), DMA((3, 6)), DMA((3, 6))],
         compiler_params=params(has_side_effects=True),
         name="experts",
     )(x_in, post, gates, *rows, w_gate, w_up, w_down)

time: 379 us -> 358 us (0.945)
  Pallas kernels: 368 us -> 346 us
    pallas_call x1, Pallas kernels: 159 us -> 145 us  [dispatch(): pl.pallas_call(dispatch_kernel, out_shape=(table, table) + tuple((shape((...]
    pallas_call x1, Pallas kernels: 206 us -> 198 us  [experts_mlp(): pl.pallas_call(expert_kernel, out_shape=(shape((tokens, hidden), BF16),)...]
where the time goes in v5:
time: 358 us; the launch traced here: 351 us
  Pallas kernels  346 us (97%)
  local copies, waits for them, and re-layouts  5.06 us (1%)
    pallas_call x1, Pallas kernels, experts_mlp(): pl.pallas_call(expert_kernel, out_shape=(shape((tokens, hidden), BF16),)...  198 us
    pallas_call x1, Pallas kernels, dispatch(): pl.pallas_call(dispatch_kernel, out_shape=(table, table) + tuple((shape((...  145 us

profile of v5, /device:TPU:2, one launch (start us, length us, event | category | flops | bytes accessed | tf_op | source)
XLA Modules:
  0.0 351.4 jit_solution(4823133621036674540)
XLA Ops:
  0.0 1.3 reshape.3.gain_ref
  1.3 1.5 copy.8.ids_ref
  2.8 3.2 route.1
  6.0 145.0 %dispatch.1 = (f32[10,128,256]{2,1,0:T(8,128)}, f32[10,128,256]{2,1,0:T(8,128)}, bf16[128,32,768]{2,1,0:T(8,128)(2,1)}, bf16[128,32,640]{2,1,0:T(8,128)(2,1)}, bf16[128,32,640]{2,1,0:T(8,128)(2,1)}) custom-call(bf16[256,2048]{1,0:T(8,128)(2,1)} %get-tuple-element.13.h_ref, s32[8,256]{1,0:T(8,128)} %bitcast.2, f32[8,256]{1,0:T(8,128)} %get-tuple-element.14.gate_ref), custom_call_target="tpu_custom_call" | custom-call | tf_op jit(solution)/shard_map/dispatch/pallas_call | solution.py:421
  151.0 198.1 %experts.1 = (bf16[256,2048]{1,0:T(8,128)(2,1)}, bf16[128,32,768]{2,1,0:T(8,128)(2,1)}, bf16[128,32,640]{2,1,0:T(8,128)(2,1)}, bf16[128,32,640]{2,1,0:T(8,128)(2,1)}) custom-call(bf16[256,2048]{1,0:T(8,128)(2,1)} %x_ref.3, f32[10,128,256]{2,1,0:T(8,128)} %get-tuple-element.15.post_ref, f32[10,128,256]{2,1,0:T(8,128)} %get-tuple-element.16.gates_ref, ...), custom_call_target="tpu_custom_call" | custom-call | tf_op jit(solution)/shard_map/experts/pallas_call | solution.py:438
  349.1 2.3 copy.10

commit v6 on v5

--- a/solution.py
+++ b/solution.py
@@ -118,13 +118,17 @@
         part, n = pl.ds(first, tokens // 2), r * SIDE + 2
         remote(line[axis].at[r * SIDE + q, part], line[axis].at[n, part], line_send.at[axis], line_recv.at[axis, n], shifted(me, (axis + 1) % 3, SIDE - q)).start()
 
+    def pass_along(axis, r, first):
+        part, n = pl.ds(first, tokens // 2), 2 * SIDE
+        remote(line[axis].at[r * SIDE, part], line[axis].at[n, part], line_send.at[axis], line_recv.at[axis, n], shifted(me, axis, SIDE - r)).start()
+
     for axis in range(3):
         for n in range(1, SIDE * SIDE):
             r, q = n // SIDE, n % SIDE
             dev = shifted(shifted(me, axis, r), (axis + 1) % 3, q)
             there = ((SIDE - r) % SIDE) * SIDE + (SIDE - q) % SIDE
             remote(ids_ref, ids_scr.at[axis, there], ids_send.at[axis], ids_recv.at[axis], dev).start()
-    for r in (2, 1, 3):
+    for r in (1, 3):
         for axis in range(3):
             n = (SIDE - r) * SIDE
             src = h_ref.at[:, pl.ds(STARTS[axis], WIDTHS[axis])]
@@ -167,6 +171,14 @@
             @pl.when((t > 0) & (t < SIDE))
             def _():
                 forward(axis, r, line[axis].at[n])
+
+            @pl.when(t == 1)
+            def _():
+                pass_along(axis, 1, tokens // 2)
+
+            @pl.when(t == 2)
+            def _():
+                pass_along(axis, 3, 0)
 
             @pl.when((t >= SIDE) & (t < 2 * SIDE))
             def _():

time: 358 us -> 361 us (level)
  Pallas kernels: 346 us -> 352 us
    pallas_call x1, Pallas kernels: 198 us -> 206 us  [experts_mlp(): pl.pallas_call(expert_kernel, out_shape=(shape((tokens, hidden), BF16),)...]
where the time goes in v6:
time: 361 us; the launch traced here: 357 us
  Pallas kernels  352 us (98%)
  local copies, waits for them, and re-layouts  5.06 us (1%)
    pallas_call x1, Pallas kernels, experts_mlp(): pl.pallas_call(expert_kernel, out_shape=(shape((tokens, hidden), BF16),)...  206 us
    pallas_call x1, Pallas kernels, dispatch(): pl.pallas_call(dispatch_kernel, out_shape=(table, table) + tuple((shape((...  142 us

profile of v6, /device:TPU:2, one launch (start us, length us, event | category | flops | bytes accessed | tf_op | source)
XLA Modules:
  0.0 356.7 jit_solution(14127143655578386735)
XLA Ops:
  0.0 1.3 reshape.3.gain_ref
  1.3 1.5 copy.8.ids_ref
  2.8 3.2 route.1
  6.0 142.4 %dispatch.1 = (f32[10,128,256]{2,1,0:T(8,128)}, f32[10,128,256]{2,1,0:T(8,128)}, bf16[128,32,768]{2,1,0:T(8,128)(2,1)}, bf16[128,32,640]{2,1,0:T(8,128)(2,1)}, bf16[128,32,640]{2,1,0:T(8,128)(2,1)}) custom-call(bf16[256,2048]{1,0:T(8,128)(2,1)} %get-tuple-element.13.h_ref, s32[8,256]{1,0:T(8,128)} %bitcast.2, f32[8,256]{1,0:T(8,128)} %get-tuple-element.14.gate_ref), custom_call_target="tpu_custom_call" | custom-call | tf_op jit(solution)/shard_map/dispatch/pallas_call | solution.py:433
  148.4 206.0 %experts.1 = (bf16[256,2048]{1,0:T(8,128)(2,1)}, bf16[128,32,768]{2,1,0:T(8,128)(2,1)}, bf16[128,32,640]{2,1,0:T(8,128)(2,1)}, bf16[128,32,640]{2,1,0:T(8,128)(2,1)}) custom-call(bf16[256,2048]{1,0:T(8,128)(2,1)} %x_ref.3, f32[10,128,256]{2,1,0:T(8,128)} %get-tuple-element.15.post_ref, f32[10,128,256]{2,1,0:T(8,128)} %get-tuple-element.16.gates_ref, ...), custom_call_target="tpu_custom_call" | custom-call | tf_op jit(solution)/shard_map/experts/pallas_call | solution.py:450
  354.4 2.3 copy.10
